TPU v7x, 256 devices: a whole 4x4x8 slice. The times are simulated.
256 devices in a mesh: pipe: 32 (over z, y_hi, core), ctx: 8 (over x, y_lo).
Axes of the slice: x: 4, y: 4 (y_hi: 2, y_lo: 2; y = y_hi * 2 + y_lo), z: 8, core: 2. Of those that a mesh axis runs over, the one named last changes fastest.
Arguments:
- query_fwd: bfloat16 [32, 1024, 4096], P('pipe', 'ctx'), may hold values from -110 to 110
- key_fwd: bfloat16 [32, 1024, 1024], P('pipe', 'ctx'), may hold values from -4.5 to 4.5
- value_fwd: bfloat16 [32, 1024, 1024], P('pipe', 'ctx'), may hold values from -6 to 6
- query_bwd: bfloat16 [32, 1024, 4096], P('pipe', 'ctx'), may hold values from -110 to 110
- key_bwd: bfloat16 [32, 1024, 1024], P('pipe', 'ctx'), may hold values from -4.5 to 4.5
- value_bwd: bfloat16 [32, 1024, 1024], P('pipe', 'ctx'), may hold values from -6 to 6
- cotangent: bfloat16 [32, 1024, 4096], P('pipe', 'ctx'), may hold values from -6 to 6
- documents: int32 [32, 2, 1024], P('pipe'), may hold values from 0 to 3, never falling along the last dimension, each value on 1 to 512 neighbouring positions
Outputs:
- attended: bfloat16 [32, 1024, 4096], P('pipe', 'ctx')
- query_grad: bfloat16 [32, 1024, 4096], P('pipe', 'ctx')
- key_grad: bfloat16 [32, 1024, 1024], P('pipe', 'ctx')
- value_grad: bfloat16 [32, 1024, 1024], P('pipe', 'ctx')
Inputs may be any that keep to these rules, and one draw needn't show every extreme that they name: Along the last dimension ids never fall; 4 documents per slab, each of 1 to 512 positions, one of exactly 512.
All inputs are finite; a program needn't handle non-finite values.
Results may differ from a plain program's by a relative error of at most 0.0085.
Values may be sent and summed in bfloat16 or wider, within the bound.
No kernel may reach another device: no remote copies, remote signals or barrier semaphores. Data moves between devices by JAX's collectives and lax.ppermute only.
A program may use at most 128 MiB of HBM per device.

v0:
```python
import jax
import jax.numpy as jnp
from jax import lax
from jax.sharding import PartitionSpec as P

QHEADS = 32
KVH = 8
HD = 128
QBLK = 128


def passed_along(value, axis, steps):
    count = lax.axis_size(axis)
    pairs = [(source, (source + steps) % count) for source in range(count)]
    return lax.ppermute(value, axis, pairs)


def cut_along(value, dim, count):
    before, after = (value.shape[:dim], value.shape[dim + 1 :])
    return jnp.moveaxis(value.reshape(*before, count, -1, *after), dim, 0)


def edges_of(length, count):
    unit = 8 if length >= 8 * count else 1
    return [length // unit * k // count * unit for k in range(1, count)]


def in_order(parts, dim):
    dims = list(parts.shape[1:])
    dims[dim] *= parts.shape[0]
    return jnp.moveaxis(parts, 0, dim).reshape(dims)


def exchange_in_pieces(value, axis, pieces, split_dim, concat_dim):
    parts = cut_along(value, split_dim, lax.axis_size(axis))
    widest = max(range(1, max(2, parts.ndim - 1)), key=lambda d: parts.shape[d])
    outs = []
    for section in jnp.split(parts, edges_of(parts.shape[widest], pieces), axis=widest):
        if section.size:
            outs.append(lax.all_to_all(section, axis, split_axis=0, concat_axis=0, tiled=True))
    return in_order(jnp.concatenate(outs, axis=widest), concat_dim)


def allowed_mask(query_places, query_documents, key_places, key_documents):
    causal = key_places[None, :] <= query_places[:, None]
    same_document = key_documents[None, :] == query_documents[:, None]
    return causal & same_document


def head_probs(query_head, key_head, allowed, score_scale):
    raw_scores = (
        jnp.einsum("rgd,kd->grk", query_head, key_head, preferred_element_type=jnp.float32)
        * score_scale
    )
    masked = jnp.where(allowed[None], raw_scores, jnp.float32(-1e30))
    row_max = jnp.max(masked, axis=-1, keepdims=True)
    exponent = jnp.exp(masked - row_max)
    return exponent / jnp.sum(exponent, axis=-1, keepdims=True)


def forward_all(
    queries, keys_all, values_all, query_places, query_documents, key_places, key_documents
):
    row_count, head_count, query_width = queries.shape
    head_size = keys_all.shape[2]
    score_scale = head_size ** (-0.5)
    block_count = row_count // QBLK
    query_blocks = queries.reshape(block_count, QBLK, head_count, query_width)
    place_blocks = query_places.reshape(block_count, QBLK)
    document_blocks = query_documents.reshape(block_count, QBLK)

    def forward_one_block(packed):
        query_block, place_block, document_block = packed
        allowed = allowed_mask(place_block, document_block, key_places, key_documents)

        def forward_one_head(head):
            query_head = lax.dynamic_index_in_dim(query_block, head, 1, False).reshape(
                QBLK, -1, head_size
            )
            key_head = lax.dynamic_index_in_dim(keys_all, head, 1, False)
            value_head = lax.dynamic_index_in_dim(values_all, head, 1, False)
            weights = head_probs(query_head, key_head, allowed, score_scale).astype(jnp.bfloat16)
            mixture = jnp.einsum(
                "grk,kd->rgd", weights, value_head, preferred_element_type=jnp.float32
            )
            return mixture.reshape(QBLK, query_width).astype(jnp.bfloat16)

        return jnp.moveaxis(
            lax.map(forward_one_head, jnp.arange(head_count, dtype=jnp.int32)), 0, 1
        )

    outcome = lax.map(forward_one_block, (query_blocks, place_blocks, document_blocks))
    return outcome.reshape(row_count, head_count, query_width)


def backward_all(
    queries, keys_all, values_all, cotan, query_places, query_documents, key_places, key_documents
):
    row_count, head_count, query_width = queries.shape
    head_size = keys_all.shape[2]
    score_scale = head_size ** (-0.5)
    block_count = row_count // QBLK
    query_blocks = queries.reshape(block_count, QBLK, head_count, query_width)
    cotan_blocks = cotan.reshape(block_count, QBLK, head_count, query_width)
    place_blocks = query_places.reshape(block_count, QBLK)
    document_blocks = query_documents.reshape(block_count, QBLK)

    def backward_one_block(totals, packed):
        query_block, cotan_block, place_block, document_block = packed
        allowed = allowed_mask(place_block, document_block, key_places, key_documents)

        def backward_one_head(head):
            query_head = lax.dynamic_index_in_dim(query_block, head, 1, False).reshape(
                QBLK, -1, head_size
            )
            cotan_head = lax.dynamic_index_in_dim(cotan_block, head, 1, False).reshape(
                QBLK, -1, head_size
            )
            key_head = lax.dynamic_index_in_dim(keys_all, head, 1, False)
            value_head = lax.dynamic_index_in_dim(values_all, head, 1, False)
            probability = head_probs(query_head, key_head, allowed, score_scale)
            weights = probability.astype(jnp.bfloat16)
            prob_grad = jnp.einsum(
                "rgd,kd->grk", cotan_head, value_head, preferred_element_type=jnp.float32
            )
            row_delta = jnp.sum(probability * prob_grad, axis=-1, keepdims=True)
            score_grad = (probability * (prob_grad - row_delta) * score_scale).astype(jnp.bfloat16)
            query_part = jnp.einsum(
                "grk,kd->rgd", score_grad, key_head, preferred_element_type=jnp.float32
            )
            key_part = jnp.einsum(
                "grk,rgd->kd", score_grad, query_head, preferred_element_type=jnp.float32
            )
            value_part = jnp.einsum(
                "grk,rgd->kd", weights, cotan_head, preferred_element_type=jnp.float32
            )
            return (
                query_part.reshape(QBLK, query_width).astype(jnp.bfloat16),
                key_part,
                value_part,
            )

        query_part, key_part, value_part = lax.map(
            backward_one_head, jnp.arange(head_count, dtype=jnp.int32)
        )
        new_totals = (
            totals[0] + jnp.moveaxis(key_part, 0, 1),
            totals[1] + jnp.moveaxis(value_part, 0, 1),
        )
        return (new_totals, jnp.moveaxis(query_part, 0, 1))

    empty_sum = jnp.zeros(keys_all.shape, jnp.float32)
    sums, query_grads = lax.scan(
        backward_one_block,
        (empty_sum, empty_sum),
        (query_blocks, cotan_blocks, place_blocks, document_blocks),
    )
    return (query_grads.reshape(row_count, head_count, query_width), sums[0], sums[1])


def on_device(query_fwd, key_fwd, value_fwd, query_bwd, key_bwd, value_bwd, cotangent, documents):
    shard_rows = query_fwd.shape[1]
    context_count = lax.axis_size("ctx")
    forward_docs = documents[0, 0]
    backward_docs = documents[0, 1]
    query_width = QHEADS // KVH * HD
    arrived = passed_along((query_fwd[0], key_fwd[0], value_fwd[0]), "pipe", 1)
    cotan_local = passed_along(cotangent[0], "pipe", -1)

    def split_heads(tensor):
        return tensor.reshape(shard_rows, context_count, KVH // context_count, -1)

    packed_fwd = jnp.concatenate(
        (split_heads(arrived[0]), split_heads(arrived[1]), split_heads(arrived[2])), axis=3
    )
    exchanged = lax.all_to_all(packed_fwd, "ctx", split_axis=1, concat_axis=0, tiled=True)
    seq_length = exchanged.shape[0]
    flat = exchanged[:, 0]
    places = jnp.arange(seq_length, dtype=jnp.int32)
    queries = flat[:, :, :query_width]
    keys_in = flat[:, :, query_width : query_width + HD]
    values_in = flat[:, :, query_width + HD :]
    outcome = forward_all(queries, keys_in, values_in, places, forward_docs, places, forward_docs)
    mixture = outcome[:, None]
    returned = lax.all_to_all(mixture, "ctx", split_axis=0, concat_axis=1, tiled=True)
    attended = returned.reshape(1, shard_rows, -1)
    packed_bwd = jnp.concatenate(
        (
            split_heads(query_bwd[0]),
            split_heads(key_bwd[0]),
            split_heads(value_bwd[0]),
            split_heads(cotan_local),
        ),
        axis=3,
    )
    exchanged = lax.all_to_all(packed_bwd, "ctx", split_axis=1, concat_axis=0, tiled=True)
    seq_length = exchanged.shape[0]
    flat = exchanged[:, 0]
    places = jnp.arange(seq_length, dtype=jnp.int32)
    queries = flat[:, :, :query_width]
    keys_in = flat[:, :, query_width : query_width + HD]
    values_in = flat[:, :, query_width + HD : query_width + 2 * HD]
    cotan_in = flat[:, :, query_width + 2 * HD :]
    query_part, key_part, value_part = backward_all(
        queries, keys_in, values_in, cotan_in, places, backward_docs, places, backward_docs
    )
    joined = jnp.concatenate(
        (query_part, key_part.astype(jnp.bfloat16), value_part.astype(jnp.bfloat16)), axis=2
    )
    grads_heads = joined[:, None]
    grads_rows = exchange_in_pieces(grads_heads, "ctx", 2, 0, 1)
    grads = (
        grads_rows[:, :, :, :query_width].reshape(shard_rows, -1),
        grads_rows[:, :, :, query_width : query_width + HD].reshape(shard_rows, -1),
        grads_rows[:, :, :, query_width + HD :].reshape(shard_rows, -1),
    )
    handed = passed_along((grads[0], grads[1], grads[2]), "pipe", -1)
    return (attended, handed[0][None], handed[1][None], handed[2][None])


def solution(mesh):
    in_specs = (
        P("pipe", "ctx", None),
        P("pipe", "ctx", None),
        P("pipe", "ctx", None),
        P("pipe", "ctx", None),
        P("pipe", "ctx", None),
        P("pipe", "ctx", None),
        P("pipe", "ctx", None),
        P("pipe", None, None),
    )
    out_specs = (
        P("pipe", "ctx", None),
        P("pipe", "ctx", None),
        P("pipe", "ctx", None),
        P("pipe", "ctx", None),
    )
    return jax.shard_map(
        on_device, mesh=mesh, in_specs=in_specs, out_specs=out_specs, check_vma=False
    )
```

profile of v0, /device:TPU:1, one launch (start us, length us, event | category | flops | bytes accessed | tf_op | source)
XLA Modules:
  0.0 346.6 jit_solution(1248638120750398765)
XLA Ops:
  7.9 12.1 %collective-permute-done.3 = bf16[128,4096]{0,1:T(8,128)(2,1)S(1)} collective-permute-done((bf16[128,4096]{0,1:T(8,128)(2,1)}, bf16[128,4096]{0,1:T(8,128)(2,1)S(1)}, u32[]{:S(2)}, u32[]{:S(2)}) %collective-permute-start.3) | collective-permute-done | bytes 1048608 | tf_op jit(solution)/shard_map/ppermute | solution.py:15
  25.2 4.8 %all-to-all-start.2 = ((bf16[128,8,1,1280]{3,0,2,1:T(8,128)(2,1)}), bf16[128,8,1,1280]{3,0,2,1:T(8,128)(2,1)S(1)}, u32[]{:S(2)}, u32[]{:S(2)}) async-start(bf16[128,8,1,1280]{3,0,2,1:T(8,128)(2,1)} %copy.122), calls=%async_computation.2 | async-start | bytes 5242880 | tf_op jit(solution)/shard_map/all_to_all | solution.py:196
  37.4 35.4 %collective-permute-done.1 = bf16[128,1024]{0,1:T(8,128)(2,1)S(1)} collective-permute-done((bf16[128,1024]{0,1:T(8,128)(2,1)S(1)}, bf16[128,1024]{0,1:T(8,128)(2,1)S(1)}, u32[]{:S(2)}, u32[]{:S(2)}) %collective-permute-start.1) | collective-permute-done | bytes 262176 | tf_op jit(solution)/shard_map/ppermute | solution.py:15
  80.9 5.1 %all-to-all-start = ((bf16[128,8,1,768]{3,0,2,1:T(8,128)(2,1)}), bf16[128,8,1,768]{3,0,2,1:T(8,128)(2,1)}, u32[]{:S(2)}, u32[]{:S(2)}) async-start(bf16[128,8,1,768]{3,0,2,1:T(8,128)(2,1)} %copy.112), calls=%async_computation | async-start | bytes 3145728 | tf_op jit(solution)/shard_map/all_to_all | solution.py:176
  88.8 152.8 %while.27 = (s32[]{:T(128)}, f32[1024,1,128]{2,0,1:T(8,128)}, f32[1024,1,128]{2,0,1:T(8,128)}, bf16[8,128,1,512]{3,1,0,2:T(8,128)(2,1)}, s32[8,128]{1,0:T(8,128)...) while((s32[]{:T(128)}, f32[1024,1,128]{2,0,1:T(8,128)}, ...), condition=%wide.region_8.9_spmd.clone, body=%wide.region_4.8_spmd.clone.sunk | while | flops 683610112 | bytes 28458696 | solution.py:153
  93.4 4.5 %convolution_convert_fusion.5 = bf16[4,128,128]{1,2,0:T(8,128)(2,1)S(1)} fusion(f32[128,4,1024]{2,0,1:T(8,128)S(1)} %fusion.100, bf16[1024,1,128]{0,2,1:T(8,128)(2,1)S(1)} %get-tuple-element.584, f32[4,128,1024]{2,1,0:T(8,128)} %get-tuple-element.521, f32[4,128]{1,0:T(4,128)S(1)} %get-tuple-element.522), kind=kOutput, calls=%fused_computation.42.clone.1 | convolution fusion | flops 137954816 | bytes 4589568 | tf_op jit(solution)/shard_map/while/body/eval_jaxpr/while/body/eval_jaxpr/grk,kd->rgd/dot_general | solution.py:128
  101.7 5.3 %fusion.105 = f32[1024,1,128]{2,0,1:T(8,128)S(1)} fusion(bf16[128,4,128]{0,2,1:T(8,128)(2,1)S(1)} %bitcast.198, f32[128,4,1024]{2,0,1:T(8,128)S(1)} %fusion.100, f32[1024,1,128]{2,0,1:T(8,128)S(1)} %copy-done.4, pred[]{:T(512)S(6)} %compare.3, f32[4,128,1024]{2,1,0:T(8,128)} %get-tuple-element.521, f32[4,128]{1,0:T(4,128)S(1)} %get-tuple-element.522), kind=kOutput, calls=%fused_computation.41.clone.1 | convolution fusion | flops 138151424 | bytes 5376001 | tf_op jit(solution)/shard_map/while/body/eval_jaxpr/while/body/eval_jaxpr/grk,rgd->kd/dot_general | solution.py:131
  112.4 4.5 %convolution_convert_fusion.5 = bf16[4,128,128]{1,2,0:T(8,128)(2,1)S(1)} fusion(f32[128,4,1024]{2,0,1:T(8,128)S(1)} %fusion.100, bf16[1024,1,128]{0,2,1:T(8,128)(2,1)S(1)} %get-tuple-element.584, f32[4,128,1024]{2,1,0:T(8,128)} %get-tuple-element.521, f32[4,128]{1,0:T(4,128)S(1)} %get-tuple-element.522), kind=kOutput, calls=%fused_computation.42.clone.1 | convolution fusion | flops 137954816 | bytes 4589568 | tf_op jit(solution)/shard_map/while/body/eval_jaxpr/while/body/eval_jaxpr/grk,kd->rgd/dot_general | solution.py:128
  120.8 5.3 %fusion.105 = f32[1024,1,128]{2,0,1:T(8,128)S(1)} fusion(bf16[128,4,128]{0,2,1:T(8,128)(2,1)S(1)} %bitcast.198, f32[128,4,1024]{2,0,1:T(8,128)S(1)} %fusion.100, f32[1024,1,128]{2,0,1:T(8,128)S(1)} %copy-done.4, pred[]{:T(512)S(6)} %compare.3, f32[4,128,1024]{2,1,0:T(8,128)} %get-tuple-element.521, f32[4,128]{1,0:T(4,128)S(1)} %get-tuple-element.522), kind=kOutput, calls=%fused_computation.41.clone.1 | convolution fusion | flops 138151424 | bytes 5376001 | tf_op jit(solution)/shard_map/while/body/eval_jaxpr/while/body/eval_jaxpr/grk,rgd->kd/dot_general | solution.py:131
  131.5 4.5 %convolution_convert_fusion.5 = bf16[4,128,128]{1,2,0:T(8,128)(2,1)S(1)} fusion(f32[128,4,1024]{2,0,1:T(8,128)S(1)} %fusion.100, bf16[1024,1,128]{0,2,1:T(8,128)(2,1)S(1)} %get-tuple-element.584, f32[4,128,1024]{2,1,0:T(8,128)} %get-tuple-element.521, f32[4,128]{1,0:T(4,128)S(1)} %get-tuple-element.522), kind=kOutput, calls=%fused_computation.42.clone.1 | convolution fusion | flops 137954816 | bytes 4589568 | tf_op jit(solution)/shard_map/while/body/eval_jaxpr/while/body/eval_jaxpr/grk,kd->rgd/dot_general | solution.py:128
  139.9 5.3 %fusion.105 = f32[1024,1,128]{2,0,1:T(8,128)S(1)} fusion(bf16[128,4,128]{0,2,1:T(8,128)(2,1)S(1)} %bitcast.198, f32[128,4,1024]{2,0,1:T(8,128)S(1)} %fusion.100, f32[1024,1,128]{2,0,1:T(8,128)S(1)} %copy-done.4, pred[]{:T(512)S(6)} %compare.3, f32[4,128,1024]{2,1,0:T(8,128)} %get-tuple-element.521, f32[4,128]{1,0:T(4,128)S(1)} %get-tuple-element.522), kind=kOutput, calls=%fused_computation.41.clone.1 | convolution fusion | flops 138151424 | bytes 5376001 | tf_op jit(solution)/shard_map/while/body/eval_jaxpr/while/body/eval_jaxpr/grk,rgd->kd/dot_general | solution.py:131
  150.6 4.5 %convolution_convert_fusion.5 = bf16[4,128,128]{1,2,0:T(8,128)(2,1)S(1)} fusion(f32[128,4,1024]{2,0,1:T(8,128)S(1)} %fusion.100, bf16[1024,1,128]{0,2,1:T(8,128)(2,1)S(1)} %get-tuple-element.584, f32[4,128,1024]{2,1,0:T(8,128)} %get-tuple-element.521, f32[4,128]{1,0:T(4,128)S(1)} %get-tuple-element.522), kind=kOutput, calls=%fused_computation.42.clone.1 | convolution fusion | flops 137954816 | bytes 4589568 | tf_op jit(solution)/shard_map/while/body/eval_jaxpr/while/body/eval_jaxpr/grk,kd->rgd/dot_general | solution.py:128
  159.0 5.3 %fusion.105 = f32[1024,1,128]{2,0,1:T(8,128)S(1)} fusion(bf16[128,4,128]{0,2,1:T(8,128)(2,1)S(1)} %bitcast.198, f32[128,4,1024]{2,0,1:T(8,128)S(1)} %fusion.100, f32[1024,1,128]{2,0,1:T(8,128)S(1)} %copy-done.4, pred[]{:T(512)S(6)} %compare.3, f32[4,128,1024]{2,1,0:T(8,128)} %get-tuple-element.521, f32[4,128]{1,0:T(4,128)S(1)} %get-tuple-element.522), kind=kOutput, calls=%fused_computation.41.clone.1 | convolution fusion | flops 138151424 | bytes 5376001 | tf_op jit(solution)/shard_map/while/body/eval_jaxpr/while/body/eval_jaxpr/grk,rgd->kd/dot_general | solution.py:131
  169.8 4.5 %convolution_convert_fusion.5 = bf16[4,128,128]{1,2,0:T(8,128)(2,1)S(1)} fusion(f32[128,4,1024]{2,0,1:T(8,128)S(1)} %fusion.100, bf16[1024,1,128]{0,2,1:T(8,128)(2,1)S(1)} %get-tuple-element.584, f32[4,128,1024]{2,1,0:T(8,128)} %get-tuple-element.521, f32[4,128]{1,0:T(4,128)S(1)} %get-tuple-element.522), kind=kOutput, calls=%fused_computation.42.clone.1 | convolution fusion | flops 137954816 | bytes 4589568 | tf_op jit(solution)/shard_map/while/body/eval_jaxpr/while/body/eval_jaxpr/grk,kd->rgd/dot_general | solution.py:128
  178.1 5.3 %fusion.105 = f32[1024,1,128]{2,0,1:T(8,128)S(1)} fusion(bf16[128,4,128]{0,2,1:T(8,128)(2,1)S(1)} %bitcast.198, f32[128,4,1024]{2,0,1:T(8,128)S(1)} %fusion.100, f32[1024,1,128]{2,0,1:T(8,128)S(1)} %copy-done.4, pred[]{:T(512)S(6)} %compare.3, f32[4,128,1024]{2,1,0:T(8,128)} %get-tuple-element.521, f32[4,128]{1,0:T(4,128)S(1)} %get-tuple-element.522), kind=kOutput, calls=%fused_computation.41.clone.1 | convolution fusion | flops 138151424 | bytes 5376001 | tf_op jit(solution)/shard_map/while/body/eval_jaxpr/while/body/eval_jaxpr/grk,rgd->kd/dot_general | solution.py:131
  197.2 5.3 %fusion.105 = f32[1024,1,128]{2,0,1:T(8,128)S(1)} fusion(bf16[128,4,128]{0,2,1:T(8,128)(2,1)S(1)} %bitcast.198, f32[128,4,1024]{2,0,1:T(8,128)S(1)} %fusion.100, f32[1024,1,128]{2,0,1:T(8,128)S(1)} %copy-done.4, pred[]{:T(512)S(6)} %compare.3, f32[4,128,1024]{2,1,0:T(8,128)} %get-tuple-element.521, f32[4,128]{1,0:T(4,128)S(1)} %get-tuple-element.522), kind=kOutput, calls=%fused_computation.41.clone.1 | convolution fusion | flops 138151424 | bytes 5376001 | tf_op jit(solution)/shard_map/while/body/eval_jaxpr/while/body/eval_jaxpr/grk,rgd->kd/dot_general | solution.py:131
  208.0 4.5 %convolution_convert_fusion.5 = bf16[4,128,128]{1,2,0:T(8,128)(2,1)S(1)} fusion(f32[128,4,1024]{2,0,1:T(8,128)S(1)} %fusion.100, bf16[1024,1,128]{0,2,1:T(8,128)(2,1)S(1)} %get-tuple-element.584, f32[4,128,1024]{2,1,0:T(8,128)} %get-tuple-element.521, f32[4,128]{1,0:T(4,128)S(1)} %get-tuple-element.522), kind=kOutput, calls=%fused_computation.42.clone.1 | convolution fusion | flops 137954816 | bytes 4589568 | tf_op jit(solution)/shard_map/while/body/eval_jaxpr/while/body/eval_jaxpr/grk,kd->rgd/dot_general | solution.py:128
  216.3 5.3 %fusion.105 = f32[1024,1,128]{2,0,1:T(8,128)S(1)} fusion(bf16[128,4,128]{0,2,1:T(8,128)(2,1)S(1)} %bitcast.198, f32[128,4,1024]{2,0,1:T(8,128)S(1)} %fusion.100, f32[1024,1,128]{2,0,1:T(8,128)S(1)} %copy-done.4, pred[]{:T(512)S(6)} %compare.3, f32[4,128,1024]{2,1,0:T(8,128)} %get-tuple-element.521, f32[4,128]{1,0:T(4,128)S(1)} %get-tuple-element.522), kind=kOutput, calls=%fused_computation.41.clone.1 | convolution fusion | flops 138151424 | bytes 5376001 | tf_op jit(solution)/shard_map/while/body/eval_jaxpr/while/body/eval_jaxpr/grk,rgd->kd/dot_general | solution.py:131
  235.4 5.3 %fusion.105 = f32[1024,1,128]{2,0,1:T(8,128)S(1)} fusion(bf16[128,4,128]{0,2,1:T(8,128)(2,1)S(1)} %bitcast.198, f32[128,4,1024]{2,0,1:T(8,128)S(1)} %fusion.100, f32[1024,1,128]{2,0,1:T(8,128)S(1)} %copy-done.4, pred[]{:T(512)S(6)} %compare.3, f32[4,128,1024]{2,1,0:T(8,128)} %get-tuple-element.521, f32[4,128]{1,0:T(4,128)S(1)} %get-tuple-element.522), kind=kOutput, calls=%fused_computation.41.clone.1 | convolution fusion | flops 138151424 | bytes 5376001 | tf_op jit(solution)/shard_map/while/body/eval_jaxpr/while/body/eval_jaxpr/grk,rgd->kd/dot_general | solution.py:131
  244.9 17.2 %all_to_all.55 = bf16[8,64,1,1,768]{4,1,3,2,0:T(8,128)(2,1)S(1)} all-to-all(bf16[8,64,1,1,768]{4,1,3,2,0:T(8,128)(2,1)S(1)} %get-tuple-element.381), channel_id=1, replica_groups=mesh['pipe'=32,'ctx'=8] {'ctx'}, dimensions={0} | all-to-all | bytes 1572864 | tf_op jit(solution)/shard_map/all_to_all | solution.py:40
  271.6 6.2 %all-to-all-done.4 = bf16[8,64,1,1,768]{4,1,3,2,0:T(8,128)(2,1)} async-done(((bf16[8,64,1,1,768]{4,1,3,2,0:T(8,128)(2,1)}), bf16[8,64,1,1,768]{4,1,3,2,0:T(8,128)(2,1)}, u32[]{:S(2)}, u32[]{:S(2)}) %all-to-all-start.4) | async-done | bytes 786464 | tf_op jit(solution)/shard_map/all_to_all | solution.py:40
  284.6 27.3 %while.26 = (s32[]{:T(128)}, bf16[8,128,1,512]{3,1,0,2:T(8,128)(2,1)S(1)}, s32[8,128]{1,0:T(8,128)S(1)}, s32[1,1,1024]{2,1,0:T(1,128)S(1)}, s32[8,128]{1,0:T(8,1...) while((s32[]{:T(128)}, ...), condition=%wide.region_3.4_spmd.clone, body=%wide.region_0.3_spmd.clone.sunk | while | flops 273089536 | bytes 10497129 | solution.py:92
  321.0 4.8 %collective-permute-start.6 = (bf16[128,1024]{0,1:T(8,128)(2,1)}, bf16[128,1024]{0,1:T(8,128)(2,1)S(1)}, u32[]{:S(2)}, u32[]{:S(2)}) collective-permute-start(bf16[128,1024]{0,1:T(8,128)(2,1)} %bitcast.41), channel_id=1, source_target_pairs={{0,248},{8,0},{16,8},{24,16},{32,24},{40,32},{48,40},{56,48},{64,5... | collective-permute-start | bytes 786440 | tf_op jit(solution)/shard_map/ppermute | solution.py:15
  325.8 12.5 %all-to-all-done.1 = bf16[8,2,32768]{2,1,0:T(2,128)(2,1)S(1)} async-done(((bf16[8,2,32768]{2,1,0:T(2,128)(2,1)}), bf16[8,2,32768]{2,1,0:T(2,128)(2,1)S(1)}, u32[]{:S(2)}, u32[]{:S(2)}) %all-to-all-start.1) | async-done | bytes 1048608 | tf_op jit(solution)/shard_map/all_to_all | solution.py:185
  (271 shorter events, 177.3 us)
Async XLA Ops:
  0.6 5.6 %copy-start.3 = (bf16[1,128,4096]{2,1,0:T(8,128)(2,1)S(1)}, bf16[1,128,4096]{2,1,0:T(8,128)(2,1)}, u32[]{:S(2)}) copy-start(bf16[1,128,4096]{2,1,0:T(8,128)(2,1)} %param.15) | copy-start | bytes 3145732
  0.6 6.9 %copy-start.6 = (bf16[1,128,1024]{2,1,0:T(8,128)(2,1)S(1)}, bf16[1,128,1024]{2,1,0:T(8,128)(2,1)}, u32[]{:S(2)}) copy-start(bf16[1,128,1024]{2,1,0:T(8,128)(2,1)} %param.16) | copy-start | bytes 786436
  0.7 7.1 %copy-start.7 = (bf16[1,128,1024]{2,1,0:T(8,128)(2,1)S(1)}, bf16[1,128,1024]{2,1,0:T(8,128)(2,1)}, u32[]{:S(2)}) copy-start(bf16[1,128,1024]{2,1,0:T(8,128)(2,1)} %param.17) | copy-start | bytes 786436
  3.0 17.0 %collective-permute-start.3 = (bf16[128,4096]{0,1:T(8,128)(2,1)}, bf16[128,4096]{0,1:T(8,128)(2,1)S(1)}, u32[]{:S(2)}, u32[]{:S(2)}) collective-permute-start(bf16[128,4096]{0,1:T(8,128)(2,1)} %bitcast.20), channel_id=1, source_target_pairs={{0,248},{8,0},{16,8},{24,16},{32,24},{40,32},{48,40},{56,48},{64,5... | collective-permute-start | bytes 3145736 | tf_op jit(solution)/shard_map/ppermute | solution.py:15
  25.2 55.7 %all-to-all-start.2 = ((bf16[128,8,1,1280]{3,0,2,1:T(8,128)(2,1)}), bf16[128,8,1,1280]{3,0,2,1:T(8,128)(2,1)S(1)}, u32[]{:S(2)}, u32[]{:S(2)}) async-start(bf16[128,8,1,1280]{3,0,2,1:T(8,128)(2,1)} %copy.122), calls=%async_computation.2 | async-start | bytes 5242880 | tf_op jit(solution)/shard_map/all_to_all | solution.py:196
  30.0 3.2 copy-start.8
  30.0 6.5 %copy-start.9 = (bf16[1,128,1024]{2,1,0:T(8,128)(2,1)S(1)}, bf16[1,128,1024]{2,1,0:T(8,128)(2,1)}, u32[]{:S(2)}) copy-start(bf16[1,128,1024]{2,1,0:T(8,128)(2,1)} %param.14) | copy-start | bytes 786436
  30.0 7.4 %copy-start.11 = (s32[1,2,1024]{2,1,0:T(2,128)S(1)}, s32[1,2,1024]{2,1,0:T(2,128)}, u32[]{:S(2)}) copy-start(s32[1,2,1024]{2,1,0:T(2,128)} %param.19) | copy-start | bytes 24580
  32.4 43.4 %collective-permute-start = (bf16[128,4096]{0,1:T(8,128)(2,1)}, bf16[128,4096]{0,1:T(8,128)(2,1)}, u32[]{:S(2)}, u32[]{:S(2)}) collective-permute-start(bf16[128,4096]{0,1:T(8,128)(2,1)} %bitcast.219), channel_id=1, source_target_pairs={{0,8},{8,16},{16,24},{24,32},{32,40},{40,48},{48,56},{56,64},{64,7... | collective-permute-start | bytes 3145736 | tf_op jit(solution)/shard_map/ppermute | solution.py:15
  33.4 39.5 %collective-permute-start.1 = (bf16[128,1024]{0,1:T(8,128)(2,1)S(1)}, bf16[128,1024]{0,1:T(8,128)(2,1)S(1)}, u32[]{:S(2)}, u32[]{:S(2)}) collective-permute-start(bf16[128,1024]{0,1:T(8,128)(2,1)S(1)} %bitcast.223), channel_id=1, source_target_pairs={{0,8},{8,16},{16,24},{24,32},{32,40},{40,48},{48,56},{56,64},{64,7... | collective-permute-start | bytes 786440 | tf_op jit(solution)/shard_map/ppermute | solution.py:15
  37.4 38.4 %collective-permute-start.2 = (bf16[128,1024]{0,1:T(8,128)(2,1)}, bf16[128,1024]{0,1:T(8,128)(2,1)S(1)}, u32[]{:S(2)}, u32[]{:S(2)}) collective-permute-start(bf16[128,1024]{0,1:T(8,128)(2,1)} %bitcast.224), channel_id=1, source_target_pairs={{0,8},{8,16},{16,24},{24,32},{32,40},{40,48},{48,56},{56,64},{64,7... | collective-permute-start | bytes 786440 | tf_op jit(solution)/shard_map/ppermute | solution.py:15
  80.9 164.1 %all-to-all-start = ((bf16[128,8,1,768]{3,0,2,1:T(8,128)(2,1)}), bf16[128,8,1,768]{3,0,2,1:T(8,128)(2,1)}, u32[]{:S(2)}, u32[]{:S(2)}) async-start(bf16[128,8,1,768]{3,0,2,1:T(8,128)(2,1)} %copy.112), calls=%async_computation | async-start | bytes 3145728 | tf_op jit(solution)/shard_map/all_to_all | solution.py:176
  117.7 3.1 copy-start.4
  136.8 3.1 copy-start.4
  155.9 3.1 copy-start.4
  175.0 3.1 copy-start.4
  194.1 3.1 copy-start.4
  213.2 3.1 copy-start.4
  232.3 3.1 copy-start.4
  262.1 15.6 %all-to-all-start.4 = ((bf16[8,64,1,1,768]{4,1,3,2,0:T(8,128)(2,1)}), bf16[8,64,1,1,768]{4,1,3,2,0:T(8,128)(2,1)}, u32[]{:S(2)}, u32[]{:S(2)}) async-start(bf16[8,64,1,1,768]{4,1,3,2,0:T(8,128)(2,1)} %get-tuple-element.382), calls=%async_computation.4 | async-start | bytes 1572864 | tf_op jit(solution)/shard_map/all_to_all | solution.py:40
  282.6 61.6 %collective-permute-start.4 = (bf16[128,4096]{0,1:T(8,128)(2,1)}, bf16[128,4096]{0,1:T(8,128)(2,1)}, u32[]{:S(2)}, u32[]{:S(2)}) collective-permute-start(bf16[128,4096]{0,1:T(8,128)(2,1)} %bitcast.36), channel_id=1, source_target_pairs={{0,248},{8,0},{16,8},{24,16},{32,24},{40,32},{48,40},{56,48},{64,5... | collective-permute-start | bytes 3145736 | tf_op jit(solution)/shard_map/ppermute | solution.py:15
  315.5 22.8 %all-to-all-start.1 = ((bf16[8,2,32768]{2,1,0:T(2,128)(2,1)}), bf16[8,2,32768]{2,1,0:T(2,128)(2,1)S(1)}, u32[]{:S(2)}, u32[]{:S(2)}) async-start(bf16[8,2,32768]{2,1,0:T(2,128)(2,1)} %reshape.275), calls=%async_computation.1 | async-start | bytes 2097152 | tf_op jit(solution)/shard_map/all_to_all | solution.py:185
  321.0 20.6 %collective-permute-start.5 = (bf16[128,1024]{0,1:T(8,128)(2,1)}, bf16[128,1024]{0,1:T(8,128)(2,1)}, u32[]{:S(2)}, u32[]{:S(2)}) collective-permute-start(bf16[128,1024]{0,1:T(8,128)(2,1)} %bitcast.39), channel_id=1, source_target_pairs={{0,248},{8,0},{16,8},{24,16},{32,24},{40,32},{48,40},{56,48},{64,5... | collective-permute-start | bytes 786440 | tf_op jit(solution)/shard_map/ppermute | solution.py:15
  321.0 22.4 %collective-permute-start.6 = (bf16[128,1024]{0,1:T(8,128)(2,1)}, bf16[128,1024]{0,1:T(8,128)(2,1)S(1)}, u32[]{:S(2)}, u32[]{:S(2)}) collective-permute-start(bf16[128,1024]{0,1:T(8,128)(2,1)} %bitcast.41), channel_id=1, source_target_pairs={{0,248},{8,0},{16,8},{24,16},{32,24},{40,32},{48,40},{56,48},{64,5... | collective-permute-start | bytes 786440 | tf_op jit(solution)/shard_map/ppermute | solution.py:15
  (13 other events, 16.8 us)
where the time goes:
time: 348 us; the launch traced here: 347 us
  matrix products  118 us (34%)
  local copies, waits for them, and re-layouts  70.4 us (20%)
  waiting for transfers between devices  69.2 us (20%)
  other arithmetic  37.6 us (11%)
  starting transfers between devices  31.9 us (9%)
  blocking collectives  17.2 us (5%)
    ppermute x7, waiting for transfers between devices, passed_along(): return lax.ppermute(value, axis, pairs)  50.5 us
    dot_general x8, matrix products, backward_one_head(): jnp.einsum('grk,rgd->kd', score_grad, query_head, preferred_element_type=...  42.4 us
    dot_general x8, matrix products, backward_one_head(): jnp.einsum('grk,kd->rgd', score_grad, key_head, preferred_element_type=jn...  35.6 us
    sub x16, other arithmetic, head_probs(): exponent = jnp.exp(masked - row_max)  25.9 us
    dot_general x8, matrix products, backward_one_head(): jnp.einsum('grk,rgd->kd', weights, cotan_head, preferred_element_type=jnp...  24.8 us
    unnamed x36, local copies, waits for them, and re-layouts  19.6 us
    dynamic_slice x40, local copies, waits for them, and re-layouts, forward_all(): lax.map(forward_one_block, (query_blocks, place_blocks, document_blocks))  18.1 us
    all_to_all x1, blocking collectives, exchange_in_pieces(): lax.all_to_all(section, axis, split_axis=0, concat_axis=0, tiled=True)  17.2 us
  transfers between devices with their start and end apart: 11, of which 5 were waited for; matrix products, arithmetic and copies ran while one was open for 59% of the time, Pallas kernels for 0%

commit v1 on v0

v1 whole, which is shorter than its diff:
```python
import jax
import jax.numpy as jnp
from jax import lax
from jax.experimental import pallas as pl
from jax.experimental.pallas import tpu as pltpu
from jax.sharding import PartitionSpec as P


QHEADS = 32
KVH = 8
HD = 128
QBLK = 128
SEQ = 1024
GROUP = QHEADS // KVH
XS = 4
SLAB_KV = KVH // XS
QW = SLAB_KV * GROUP * HD
KW = SLAB_KV * HD
REACH = 4
MASKED = -1e30
SCALE = HD**-0.5
EXP2_SCALE = SCALE * 1.4426950408889634
F32 = jnp.float32
BF16 = jnp.bfloat16


def nt(a, b):
    return lax.dot_general(a, b, (((1,), (1,)), ((), ())), preferred_element_type=F32)


def nn(a, b):
    return lax.dot_general(a, b, (((1,), (0,)), ((), ())), preferred_element_type=F32)


def tn(a, b):
    return lax.dot_general(a, b, (((0,), (0,)), ((), ())), preferred_element_type=F32)


def place():
    rank = lax.axis_index("ctx")
    return rank // 2, rank % 2


def vmem_call(body, outs, scratch=()):
    return pl.pallas_call(
        body,
        out_shape=outs,
        scratch_shapes=scratch,
        compiler_params=pltpu.CompilerParams(vmem_limit_bytes=20 * 1024 * 1024),
    )


def cut_body(*refs):
    in_refs, (out_ref, held_ref, in_sems, out_sems) = refs[:-4], refs[-4:]
    loads = []
    for slab in range(XS):
        at, row = 0, []
        for n, ref in enumerate(in_refs):
            width = ref.shape[2] // XS
            source = ref.at[0, :, slab * width : (slab + 1) * width]
            target = held_ref.at[slab, :, at : at + width]
            row.append(pltpu.make_async_copy(source, target, in_sems.at[slab, n]))
            at += width
        loads.append(row)
    for row in loads:
        for load in row:
            load.start()
    stores = []
    for slab, row in enumerate(loads):
        for load in row:
            load.wait()
        stores.append(
            pltpu.make_async_copy(held_ref.at[slab], out_ref.at[slab], out_sems.at[slab])
        )
        stores[-1].start()
    for store in stores:
        store.wait()


def cut(*arrays):
    width = sum(a.shape[2] for a in arrays) // XS
    shape = (XS, QBLK, width)
    return pl.pallas_call(
        cut_body,
        in_specs=[pl.BlockSpec(memory_space=pl.ANY)] * len(arrays),
        out_specs=pl.BlockSpec(memory_space=pl.ANY),
        out_shape=jax.ShapeDtypeStruct(shape, BF16),
        scratch_shapes=[
            pltpu.VMEM(shape, BF16),
            pltpu.SemaphoreType.DMA((XS, len(arrays))),
            pltpu.SemaphoreType.DMA((XS,)),
        ],
    )(*arrays)


def turned_body(in_ref, *refs):
    out_refs, sems = refs[:XS], refs[XS]
    x, _ = place()
    width = in_ref.shape[2] // XS
    loads = []
    for k in range(XS):
        start = pl.multiple_of(lax.rem(x + k, XS) * width, width)
        source = in_ref.at[0, :, pl.ds(start, width)]
        loads.append(pltpu.make_async_copy(source, out_refs[k], sems.at[k]))
        loads[-1].start()
    for load in loads:
        load.wait()


def turned(array):
    width = array.shape[2] // XS
    return pl.pallas_call(
        turned_body,
        in_specs=[pl.BlockSpec(memory_space=pl.ANY)],
        out_specs=[pl.BlockSpec(memory_space=pltpu.VMEM)] * XS,
        out_shape=[jax.ShapeDtypeStruct((QBLK, width), BF16)] * XS,
        scratch_shapes=[pltpu.SemaphoreType.DMA((XS,))],
    )(array)


def joined_body(*refs):
    x, _ = place()
    out_ref, width = refs[XS], refs[0].shape[1]
    for k in range(XS):
        start = pl.multiple_of(lax.rem(x - k + XS, XS) * width, width)
        out_ref[0, :, pl.ds(start, width)] = refs[k][...]


def joined(parts):
    width = parts[0].shape[1]
    return vmem_call(joined_body, jax.ShapeDtypeStruct((1, QBLK, XS * width), BF16))(*parts)


def joined_grads_body(*refs):
    x, _ = place()
    mine, theirs, (dq_ref, dk_ref, dv_ref) = refs[:XS], refs[XS : 2 * XS], refs[2 * XS :]
    for k in range(XS):
        slab = lax.rem(x - k + XS, XS)
        wide = pl.multiple_of(slab * QW, QW)
        start = pl.multiple_of(slab * KW, KW)
        dq_ref[0, :, pl.ds(wide, QW)] = mine[k][:, :QW]
        total = mine[k][:, QW:].astype(F32) + theirs[k][...].astype(F32)
        dk_ref[0, :, pl.ds(start, KW)] = total[:, :KW].astype(BF16)
        dv_ref[0, :, pl.ds(start, KW)] = total[:, KW:].astype(BF16)


def joined_grads(mine, theirs):
    shape = jax.ShapeDtypeStruct((1, QBLK, XS * KW), BF16)
    wide = jax.ShapeDtypeStruct((1, QBLK, XS * QW), BF16)
    return vmem_call(joined_grads_body, (wide, shape, shape))(*mine, *theirs)


def sent_turned(parts, steps, flip=0):
    count, outs = lax.axis_size("pipe"), []
    for k in range(XS):
        pairs = []
        for p in range(count):
            for c in range(2 * XS):
                target = (c // 2 + k) % XS * 2 + (c + flip) % 2
                pairs.append((p * 2 * XS + c, (p + steps) % count * 2 * XS + target))
        outs.append(lax.ppermute(parts[k], ("pipe", "ctx"), pairs))
    return outs


def across(value):
    return lax.ppermute(value, "ctx", [(c, c ^ 1) for c in range(2 * XS)])


def over_x(value):
    evens = [2 * x for x in range(XS)]
    odds = [2 * x + 1 for x in range(XS)]
    return lax.all_to_all(
        value, "ctx", split_axis=0, concat_axis=0, axis_index_groups=[evens, odds], tiled=True
    )


def window_of(i, y):
    blocks = min(2 * i + 2, REACH + 1)
    start = 0 if blocks <= REACH else (2 * i - REACH + y)
    return blocks * QBLK, start


def fill_window(y, base, own_ref, other_ref, k_ref, v_ref):
    for i in range(XS):
        own = pl.multiple_of((2 * i + y) * QBLK, QBLK)
        other = pl.multiple_of((2 * i + 1 - y) * QBLK, QBLK)
        k_ref[pl.ds(own, QBLK), :] = own_ref[i, :, base : base + KW]
        v_ref[pl.ds(own, QBLK), :] = own_ref[i, :, base + KW : base + 2 * KW]
        k_ref[pl.ds(other, QBLK), :] = other_ref[i, :, :KW]
        v_ref[pl.ds(other, QBLK), :] = other_ref[i, :, KW:]


def fill_docs(docs_ref, which, col_ref, row_ref):
    for b in range(SEQ // QBLK):
        row = docs_ref[0, which : which + 1, b * QBLK : (b + 1) * QBLK].astype(F32)
        row_ref[b] = jnp.broadcast_to(row, (8, QBLK))
        col_ref[b * QBLK : (b + 1) * QBLK, :] = jnp.broadcast_to(row, (QBLK, QBLK)).T


def fill_bias(i, y, col_ref, row_ref, bias_ref):
    length, start = window_of(i, y)
    first = pl.multiple_of(start * QBLK, QBLK)
    key_docs = col_ref[pl.ds(first, length), :]
    query_docs = row_ref[2 * i + y][:1]
    key_places = first + lax.broadcasted_iota(jnp.int32, (length, QBLK), 0)
    query_places = (2 * i + y) * QBLK + lax.broadcasted_iota(jnp.int32, (length, QBLK), 1)
    seen = (key_places <= query_places) & (key_docs == query_docs)
    bias_ref[:length, :] = jnp.where(seen, F32(0), F32(MASKED))


def stacked(ref, i, base):
    return jnp.concatenate(
        [ref[i, :, base + h * HD : base + (h + 1) * HD] for h in range(GROUP)], axis=0
    )


def probs_of(scores, bias):
    masked = scores + jnp.concatenate([bias] * GROUP, axis=1)
    row_max = jnp.max(masked, axis=0, keepdims=True)
    exponent = jnp.exp2((masked - row_max) * F32(EXP2_SCALE))
    return exponent * (1.0 / jnp.sum(exponent, axis=0, keepdims=True))


def forward_body(q0, q1, q2, q3, own_ref, other_ref, docs_ref, *refs):
    out_refs, (q_ref, mixed_ref, k_ref, v_ref, col_ref, row_ref, bias_ref) = refs[:XS], refs[XS:]
    x, y = place()
    for k, chunk in enumerate((q0, q1, q2, q3)):
        q_ref[lax.rem(x - k + XS, XS)] = chunk[...]
    fill_window(y, 2 * KW, own_ref, other_ref, k_ref, v_ref)
    fill_docs(docs_ref, 0, col_ref, row_ref)
    for i in range(XS):
        length, start = window_of(i, y)
        first = pl.multiple_of(start * QBLK, QBLK)
        fill_bias(i, y, col_ref, row_ref, bias_ref)
        for g in range(SLAB_KV):
            keys = k_ref[pl.ds(first, length), g * HD : (g + 1) * HD]
            values = v_ref[pl.ds(first, length), g * HD : (g + 1) * HD]
            queries = stacked(q_ref, i, g * GROUP * HD)
            weights = probs_of(nt(keys, queries), bias_ref[:length, :]).astype(BF16)
            mixed = tn(values, weights)
            for h in range(GROUP):
                col = (g * GROUP + h) * HD
                part = mixed[:, h * QBLK : (h + 1) * QBLK].T
                mixed_ref[i, :, col : col + HD] = part.astype(BF16)
    for k in range(XS):
        out_refs[k][...] = mixed_ref[lax.rem(x + k, XS)]


def forward(q, own, other, docs):
    return vmem_call(
        forward_body,
        (jax.ShapeDtypeStruct((QBLK, QW), BF16),) * XS,
        (
            pltpu.VMEM((XS, QBLK, QW), BF16),
            pltpu.VMEM((XS, QBLK, QW), BF16),
            pltpu.VMEM((SEQ, KW), BF16),
            pltpu.VMEM((SEQ, KW), BF16),
            pltpu.VMEM((SEQ, QBLK), F32),
            pltpu.VMEM((SEQ // QBLK, 8, QBLK), F32),
            pltpu.VMEM(((REACH + 1) * QBLK, QBLK), F32),
        ),
    )(*q, own, other, docs)


def backward_body(q_ref, g0, g1, g2, g3, own_ref, other_ref, docs_ref, *refs):
    mine_refs, theirs_refs = refs[:XS], refs[XS : 2 * XS]
    g_ref, dq_ref, k_ref, v_ref, col_ref, row_ref, bias_ref, dk_ref, dv_ref = refs[2 * XS :]
    x, y = place()
    for k, chunk in enumerate((g0, g1, g2, g3)):
        g_ref[lax.rem(x - k + XS, XS)] = chunk[...]
    fill_window(y, 0, own_ref, other_ref, k_ref, v_ref)
    fill_docs(docs_ref, 1, col_ref, row_ref)
    dk_ref[...] = jnp.zeros_like(dk_ref)
    dv_ref[...] = jnp.zeros_like(dv_ref)
    for i in range(XS):
        length, start = window_of(i, y)
        first = pl.multiple_of(start * QBLK, QBLK)
        fill_bias(i, y, col_ref, row_ref, bias_ref)
        for g in range(SLAB_KV):
            span = (pl.ds(first, length), slice(g * HD, (g + 1) * HD))
            keys, values = k_ref[span], v_ref[span]
            queries = stacked(q_ref, i, g * GROUP * HD)
            cotan = stacked(g_ref, i, g * GROUP * HD)
            probs = probs_of(nt(keys, queries), bias_ref[:length, :])
            prob_grad = nt(values, cotan)
            delta = jnp.sum(probs * prob_grad, axis=0, keepdims=True)
            score_grad = (probs * (prob_grad - delta) * F32(SCALE)).astype(BF16)
            dv_ref[span] += nn(probs.astype(BF16), cotan)
            dk_ref[span] += nn(score_grad, queries)
            dq = tn(keys, score_grad)
            for h in range(GROUP):
                col = (g * GROUP + h) * HD
                part = dq[:, h * QBLK : (h + 1) * QBLK].T
                dq_ref[i, :, col : col + HD] = part.astype(BF16)
    for k in range(XS):
        i = lax.rem(x + k, XS)
        own = pl.multiple_of((2 * i + y) * QBLK, QBLK)
        other = pl.multiple_of((2 * i + 1 - y) * QBLK, QBLK)
        mine_refs[k][:, :QW] = dq_ref[i]
        mine_refs[k][:, QW : QW + KW] = dk_ref[pl.ds(own, QBLK), :].astype(BF16)
        mine_refs[k][:, QW + KW :] = dv_ref[pl.ds(own, QBLK), :].astype(BF16)
        theirs_refs[k][:, :KW] = dk_ref[pl.ds(other, QBLK), :].astype(BF16)
        theirs_refs[k][:, KW:] = dv_ref[pl.ds(other, QBLK), :].astype(BF16)


def backward(q, g, own, other, docs):
    outs = vmem_call(
        backward_body,
        (jax.ShapeDtypeStruct((QBLK, QW + 2 * KW), BF16),) * XS
        + (jax.ShapeDtypeStruct((QBLK, 2 * KW), BF16),) * XS,
        (
            pltpu.VMEM((XS, QBLK, QW), BF16),
            pltpu.VMEM((XS, QBLK, QW), BF16),
            pltpu.VMEM((SEQ, KW), BF16),
            pltpu.VMEM((SEQ, KW), BF16),
            pltpu.VMEM((SEQ, QBLK), F32),
            pltpu.VMEM((SEQ // QBLK, 8, QBLK), F32),
            pltpu.VMEM(((REACH + 1) * QBLK, QBLK), F32),
            pltpu.VMEM((SEQ, KW), F32),
            pltpu.VMEM((SEQ, KW), F32),
        ),
    )(q, *g, own, other, docs)
    return outs[:XS], outs[XS:]


def shifted(value, steps):
    count = lax.axis_size("pipe")
    return lax.ppermute(value, "pipe", [(p, (p + steps) % count) for p in range(count)])


def on_device(query_fwd, key_fwd, value_fwd, query_bwd, key_bwd, value_bwd, cotangent, documents):
    own = over_x(cut(key_bwd, value_bwd, key_fwd, value_fwd))
    cotan = sent_turned(turned(cotangent), -1)
    docs_fwd = shifted(documents, -1)
    kv_bwd = across(own[:, :, : 2 * KW])
    kv_fwd = across(own[:, :, 2 * KW :])
    queries_bwd = over_x(cut(query_bwd))
    queries_fwd = sent_turned(turned(query_fwd), 0)
    mine, theirs = backward(queries_bwd, cotan, own, kv_bwd, documents)
    mine = sent_turned(mine, -1)
    theirs = sent_turned(theirs, -1, 1)
    mixed = forward(queries_fwd, own, kv_fwd, docs_fwd)
    mixed = sent_turned(mixed, 1)
    return joined(mixed), *joined_grads(mine, theirs)


def solution(mesh):
    rows = P("pipe", "ctx", None)
    return jax.shard_map(
        on_device,
        mesh=mesh,
        in_specs=(rows,) * 7 + (P("pipe", None, None),),
        out_specs=(rows,) * 4,
        check_vma=False,
    )
```

time: 348 us -> 144 us (0.41)
  the two profiles are of different devices: /device:TPU:1 before, /device:TPU:32 now
where the time goes in v1:
time: 144 us
  starting transfers between devices  57.9 us (40%)
  waiting for transfers between devices  56.9 us (40%)
  Pallas kernels  27.1 us (19%)
    ppermute x20, starting transfers between devices, sent_turned(): outs.append(lax.ppermute(parts[k], ('pipe', 'ctx'), pairs))  46.3 us
    ppermute x20, waiting for transfers between devices, sent_turned(): outs.append(lax.ppermute(parts[k], ('pipe', 'ctx'), pairs))  46 us
    all_to_all x2, waiting for transfers between devices, over_x(): lax.all_to_all(value, 'ctx', split_axis=0, concat_axis=0, axis_index_grou...  10.9 us
    pallas_call x1, Pallas kernels, backward(): vmem_call(backward_body, (jax.ShapeDtypeStruct((QBLK, QW + 2 * KW), BF16)...  10.1 us
    all_to_all x2, starting transfers between devices, over_x(): lax.all_to_all(value, 'ctx', split_axis=0, concat_axis=0, axis_index_grou...  7.82 us
    pallas_call x1, Pallas kernels, forward(): vmem_call(forward_body, (jax.ShapeDtypeStruct((QBLK, QW), BF16),) * XS, (...  6.23 us
    pallas_call x2, Pallas kernels, turned(): pl.pallas_call(turned_body, in_specs=[pl.BlockSpec(memory_space=pl.ANY)],...  4.39 us
    pallas_call x2, Pallas kernels, cut(): pl.pallas_call(cut_body, in_specs=[pl.BlockSpec(memory_space=pl.ANY)] * l...  4.11 us
  transfers between devices with their start and end apart: 25, of which 7 were waited for; matrix products, arithmetic and copies ran while one was open for 1% of the time, Pallas kernels for 17%

profile of v1, /device:TPU:32, one launch (start us, length us, event | category | flops | bytes accessed | tf_op | source)
XLA Modules:
  0.0 143.7 jit_solution(17342396658680381199)
XLA Ops:
  0.6 2.1 %shard_map.112 = bf16[4,128,1024]{2,1,0:T(8,128)(2,1)} custom-call(bf16[1,128,1024]{2,1,0:T(8,128)(2,1)} %refs_0_.2, bf16[1,128,1024]{2,1,0:T(8,128)(2,1)} %refs_1_.1, bf16[1,128,1024]{2,1,0:T(8,128)(2,1)} %refs_2_.1, bf16[1,128,1024]{2,1,0:T(8,128)(2,1)} %refs_3_.1), custom_call_target="tpu_custom_call" | custom-call | tf_op jit(solution)/shard_map/pallas_call | solution.py:83
  2.8 4.3 %all-to-all-start = ((bf16[4,128,1024]{2,1,0:T(8,128)(2,1)}), bf16[4,128,1024]{2,1,0:T(8,128)(2,1)S(1)}, u32[]{:S(2)}, u32[]{:S(2)}) async-start(bf16[4,128,1024]{2,1,0:T(8,128)(2,1)} %shard_map.112), calls=%async_computation | async-start | bytes 2097152 | tf_op jit(solution)/shard_map/all_to_all | solution.py:172
  7.1 2.2 %shard_map.116 = (bf16[128,1024]{1,0:T(8,128)(2,1)}, bf16[128,1024]{1,0:T(8,128)(2,1)}, bf16[128,1024]{1,0:T(8,128)(2,1)}, bf16[128,1024]{1,0:T(8,128)(2,1)}) custom-call(bf16[1,128,4096]{2,1,0:T(8,128)(2,1)} %in_ref.3), custom_call_target="tpu_custom_call" | custom-call | tf_op jit(solution)/shard_map/pallas_call | solution.py:112
  9.3 2.0 %shard_map.115 = bf16[4,128,1024]{2,1,0:T(8,128)(2,1)} custom-call(bf16[1,128,4096]{2,1,0:T(8,128)(2,1)} %refs_0_.3), custom_call_target="tpu_custom_call" | custom-call | tf_op jit(solution)/shard_map/pallas_call | solution.py:83
  11.3 10.9 %all-to-all-done.own_ref = bf16[4,128,1024]{2,1,0:T(8,128)(2,1)S(1)} async-done(((bf16[4,128,1024]{2,1,0:T(8,128)(2,1)}), bf16[4,128,1024]{2,1,0:T(8,128)(2,1)S(1)}, u32[]{:S(2)}, u32[]{:S(2)}) %all-to-all-start) | async-done | bytes 1048608 | tf_op jit(solution)/shard_map/all_to_all | solution.py:172
  22.2 3.5 %all-to-all-start.1 = ((bf16[4,128,1024]{2,1,0:T(8,128)(2,1)}), bf16[4,128,1024]{2,1,0:T(8,128)(2,1)S(1)}, u32[]{:S(2)}, u32[]{:S(2)}) async-start(bf16[4,128,1024]{2,1,0:T(8,128)(2,1)} %shard_map.115), calls=%async_computation.1 | async-start | bytes 2097152 | tf_op jit(solution)/shard_map/all_to_all | solution.py:172
  28.8 2.1 %collective-permute-start.5 = (s32[1,2,1024]{2,1,0:T(2,128)S(1)}, s32[1,2,1024]{2,1,0:T(2,128)S(1)}, u32[]{:S(2)}, u32[]{:S(2)}) collective-permute-start(s32[1,2,1024]{2,1,0:T(2,128)S(1)} %copy-done), channel_id=1, source_target_pairs={{0,248},{8,0},{16,8},{24,16},{32,24},{40,32},{48,40},{56,48},{64,5... | collective-permute-start | bytes 24584 | tf_op jit(solution)/shard_map/ppermute | solution.py:328
  32.4 2.9 %collective-permute-start.12 = (bf16[128,1024]{1,0:T(8,128)(2,1)}, bf16[128,1024]{1,0:T(8,128)(2,1)}, u32[]{:S(2)}, u32[]{:S(2)}) collective-permute-start(bf16[128,1024]{1,0:T(8,128)(2,1)} %get-tuple-element.37), channel_id=1, source_target_pairs={{0,252},{1,253},{2,254},{3,255},{4,248},{5,249},{6,250},{7,251},{8... | collective-permute-start | bytes 786440 | tf_op jit(solution)/shard_map/ppermute | solution.py:161
  35.4 6.8 %collective-permute-start.13 = (bf16[128,1024]{1,0:T(8,128)(2,1)}, bf16[128,1024]{1,0:T(8,128)(2,1)}, u32[]{:S(2)}, u32[]{:S(2)}) collective-permute-start(bf16[128,1024]{1,0:T(8,128)(2,1)} %get-tuple-element.38), channel_id=1, source_target_pairs={{0,254},{1,255},{2,248},{3,249},{4,250},{5,251},{6,252},{7,253},{8... | collective-permute-start | bytes 786440 | tf_op jit(solution)/shard_map/ppermute | solution.py:161
  42.3 2.2 %shard_map.111 = (bf16[128,1024]{1,0:T(8,128)(2,1)}, bf16[128,1024]{1,0:T(8,128)(2,1)}, bf16[128,1024]{1,0:T(8,128)(2,1)}, bf16[128,1024]{1,0:T(8,128)(2,1)}) custom-call(bf16[1,128,4096]{2,1,0:T(8,128)(2,1)} %in_ref.2), custom_call_target="tpu_custom_call" | custom-call | tf_op jit(solution)/shard_map/pallas_call | solution.py:112
  44.5 3.6 %collective-permute-done.11.g1 = bf16[128,1024]{1,0:T(8,128)(2,1)} collective-permute-done((bf16[128,1024]{1,0:T(8,128)(2,1)}, bf16[128,1024]{1,0:T(8,128)(2,1)}, u32[]{:S(2)}, u32[]{:S(2)}) %collective-permute-start.11) | collective-permute-done | bytes 262176 | tf_op jit(solution)/shard_map/ppermute | solution.py:161
  48.1 2.9 %collective-permute-start = (bf16[128,1024]{1,0:T(8,128)(2,1)}, bf16[128,1024]{1,0:T(8,128)(2,1)}, u32[]{:S(2)}, u32[]{:S(2)}) collective-permute-start(bf16[128,1024]{1,0:T(8,128)(2,1)} %get-tuple-element.27), channel_id=1, source_target_pairs={{0,0},{1,1},{2,2},{3,3},{4,4},{5,5},{6,6},{7,7},{8,8},{9,9},{10,10... | collective-permute-start | bytes 786440 | tf_op jit(solution)/shard_map/ppermute | solution.py:161
  51.3 7.6 %collective-permute-done.13.g3 = bf16[128,1024]{1,0:T(8,128)(2,1)} collective-permute-done((bf16[128,1024]{1,0:T(8,128)(2,1)}, bf16[128,1024]{1,0:T(8,128)(2,1)}, u32[]{:S(2)}, u32[]{:S(2)}) %collective-permute-start.13) | collective-permute-done | bytes 262176 | tf_op jit(solution)/shard_map/ppermute | solution.py:161
  60.1 10.1 %shard_map.117 = (bf16[128,1536]{1,0:T(8,128)(2,1)S(1)}, bf16[128,1536]{1,0:T(8,128)(2,1)S(1)}, bf16[128,1536]{1,0:T(8,128)(2,1)S(1)}, bf16[128,1536]{1,0:T(8,12...) custom-call(bf16[4,128,1024]{2,1,0:T(8,128)(2,1)S(1)} %all-to-all-do, ...), custom_call_target="tpu_custom_call" | custom-call | tf_op jit(solution)/shard_map/pallas_call | solution.py:307
  70.2 2.1 %collective-permute-start.19 = (bf16[128,512]{1,0:T(8,128)(2,1)S(1)}, bf16[128,512]{1,0:T(8,128)(2,1)S(1)}, u32[]{:S(2)}, u32[]{:S(2)}) collective-permute-start(bf16[128,512]{1,0:T(8,128)(2,1)S(1)} %get-tuple-element.43), channel_id=1, source_target_pairs={{0,249},{1,248},{2,251},{3,250},{4,253},{5,252},{6,255},{7,254},{8... | collective-permute-start | bytes 393224 | tf_op jit(solution)/shard_map/ppermute | solution.py:161
  72.3 6.2 %shard_map.113 = (bf16[128,1024]{1,0:T(8,128)(2,1)S(1)}, bf16[128,1024]{1,0:T(8,128)(2,1)S(1)}, bf16[128,1024]{1,0:T(8,128)(2,1)S(1)}, bf16[128,1024]{1,0:T(8,128)(2,1)S(1)}) custom-call(bf16[128,1024]{1,0:T(8,128)(2,1)} %collective-permute-done.q0, bf16[128,1024]{1,0:T(8,128)(2,1)} %collective-permute-done.1.q1, ...), custom_call_target="tpu_custom_call" | custom-call | tf_op jit(solution)/shard_map/pallas_call | solution.py:250
  78.6 3.0 %collective-permute-start.6 = (bf16[128,1024]{1,0:T(8,128)(2,1)S(1)}, bf16[128,1024]{1,0:T(8,128)(2,1)S(1)}, u32[]{:S(2)}, u32[]{:S(2)}) collective-permute-start(bf16[128,1024]{1,0:T(8,128)(2,1)S(1)} %get-tuple-element.31), channel_id=1, source_target_pairs={{0,8},{1,9},{2,10},{3,11},{4,12},{5,13},{6,14},{7,15},{8,16},{9,17... | collective-permute-start | bytes 786440 | tf_op jit(solution)/shard_map/ppermute | solution.py:161
  83.1 2.9 %collective-permute-start.8 = (bf16[128,1024]{1,0:T(8,128)(2,1)S(1)}, bf16[128,1024]{1,0:T(8,128)(2,1)S(1)}, u32[]{:S(2)}, u32[]{:S(2)}) collective-permute-start(bf16[128,1024]{1,0:T(8,128)(2,1)S(1)} %get-tuple-element.33), channel_id=1, source_target_pairs={{0,12},{1,13},{2,14},{3,15},{4,8},{5,9},{6,10},{7,11},{8,20},{9,21... | collective-permute-start | bytes 786440 | tf_op jit(solution)/shard_map/ppermute | solution.py:161
  86.0 5.2 %collective-permute-start.20 = (bf16[128,512]{1,0:T(8,128)(2,1)S(1)}, bf16[128,512]{1,0:T(8,128)(2,1)S(1)}, u32[]{:S(2)}, u32[]{:S(2)}) collective-permute-start(bf16[128,512]{1,0:T(8,128)(2,1)S(1)} %get-tuple-element.44), channel_id=1, source_target_pairs={{0,251},{1,250},{2,253},{3,252},{4,255},{5,254},{6,249},{7,248},{8... | collective-permute-start | bytes 393224 | tf_op jit(solution)/shard_map/ppermute | solution.py:161
  91.2 14.0 %collective-permute-done.20.refs_5_ = bf16[128,512]{1,0:T(8,128)(2,1)S(1)} collective-permute-done((bf16[128,512]{1,0:T(8,128)(2,1)S(1)}, bf16[128,512]{1,0:T(8,128)(2,1)S(1)}, u32[]{:S(2)}, u32[]{:S(2)}) %collective-permute-start.20) | collective-permute-done | bytes 131104 | tf_op jit(solution)/shard_map/ppermute | solution.py:161
  105.3 2.9 %collective-permute-start.9 = (bf16[128,1024]{1,0:T(8,128)(2,1)S(1)}, bf16[128,1024]{1,0:T(8,128)(2,1)S(1)}, u32[]{:S(2)}, u32[]{:S(2)}) collective-permute-start(bf16[128,1024]{1,0:T(8,128)(2,1)S(1)} %get-tuple-element.34), channel_id=1, source_target_pairs={{0,14},{1,15},{2,8},{3,9},{4,10},{5,11},{6,12},{7,13},{8,22},{9,23... | collective-permute-start | bytes 786440 | tf_op jit(solution)/shard_map/ppermute | solution.py:161
  110.5 5.1 %collective-permute-done.9.refs_3_ = bf16[128,1024]{1,0:T(8,128)(2,1)S(1)} collective-permute-done((bf16[128,1024]{1,0:T(8,128)(2,1)S(1)}, bf16[128,1024]{1,0:T(8,128)(2,1)S(1)}, u32[]{:S(2)}, u32[]{:S(2)}) %collective-permute-start.9) | collective-permute-done | bytes 262176 | tf_op jit(solution)/shard_map/ppermute | solution.py:161
  115.7 10.4 %collective-permute-start.22 = (bf16[128,512]{1,0:T(8,128)(2,1)S(1)}, bf16[128,512]{1,0:T(8,128)(2,1)S(1)}, u32[]{:S(2)}, u32[]{:S(2)}) collective-permute-start(bf16[128,512]{1,0:T(8,128)(2,1)S(1)} %get-tuple-element.46), channel_id=1, source_target_pairs={{0,255},{1,254},{2,249},{3,248},{4,251},{5,250},{6,253},{7,252},{8... | collective-permute-start | bytes 393224 | tf_op jit(solution)/shard_map/ppermute | solution.py:161
  127.1 15.4 %collective-permute-done.22.refs_7_ = bf16[128,512]{1,0:T(8,128)(2,1)S(1)} collective-permute-done((bf16[128,512]{1,0:T(8,128)(2,1)S(1)}, bf16[128,512]{1,0:T(8,128)(2,1)S(1)}, u32[]{:S(2)}, u32[]{:S(2)}) %collective-permute-start.22) | collective-permute-done | bytes 131104 | tf_op jit(solution)/shard_map/ppermute | solution.py:161
  (39 shorter events, 12.3 us)
Async XLA Ops:
  2.8 19.4 %all-to-all-start = ((bf16[4,128,1024]{2,1,0:T(8,128)(2,1)}), bf16[4,128,1024]{2,1,0:T(8,128)(2,1)S(1)}, u32[]{:S(2)}, u32[]{:S(2)}) async-start(bf16[4,128,1024]{2,1,0:T(8,128)(2,1)} %shard_map.112), calls=%async_computation | async-start | bytes 2097152 | tf_op jit(solution)/shard_map/all_to_all | solution.py:172
  22.2 37.9 %all-to-all-start.1 = ((bf16[4,128,1024]{2,1,0:T(8,128)(2,1)}), bf16[4,128,1024]{2,1,0:T(8,128)(2,1)S(1)}, u32[]{:S(2)}, u32[]{:S(2)}) async-start(bf16[4,128,1024]{2,1,0:T(8,128)(2,1)} %shard_map.115), calls=%async_computation.1 | async-start | bytes 2097152 | tf_op jit(solution)/shard_map/all_to_all | solution.py:172
  26.8 33.3 %collective-permute-start.14 = (bf16[4,128,512]{2,1,0:T(8,128)(2,1)}, bf16[4,128,512]{2,1,0:T(8,128)(2,1)S(1)}, u32[]{:S(2)}, u32[]{:S(2)}) collective-permute-start(bf16[4,128,512]{2,1,0:T(8,128)(2,1)} %get-tuple-element.50), channel_id=1, source_target_pairs={{0,1},{1,0},{2,3},{3,2},{4,5},{5,4},{6,7},{7,6},{8,9},{9,8},{10,11... | collective-permute-start | bytes 1572872 | tf_op jit(solution)/shard_map/ppermute | solution.py:166
  28.4 13.8 %collective-permute-start.10 = (bf16[128,1024]{1,0:T(8,128)(2,1)S(1)}, bf16[128,1024]{1,0:T(8,128)(2,1)S(1)}, u32[]{:S(2)}, u32[]{:S(2)}) collective-permute-start(bf16[128,1024]{1,0:T(8,128)(2,1)S(1)} %copy-done.1), channel_id=1, source_target_pairs={{0,248},{1,249},{2,250},{3,251},{4,252},{5,253},{6,254},{7,255},{8... | collective-permute-start | bytes 786440 | tf_op jit(solution)/shard_map/ppermute | solution.py:161
  30.9 17.2 %collective-permute-start.11 = (bf16[128,1024]{1,0:T(8,128)(2,1)}, bf16[128,1024]{1,0:T(8,128)(2,1)}, u32[]{:S(2)}, u32[]{:S(2)}) collective-permute-start(bf16[128,1024]{1,0:T(8,128)(2,1)} %get-tuple-element.36), channel_id=1, source_target_pairs={{0,250},{1,251},{2,252},{3,253},{4,254},{5,255},{6,248},{7,249},{8... | collective-permute-start | bytes 786440 | tf_op jit(solution)/shard_map/ppermute | solution.py:161
  32.4 18.9 %collective-permute-start.12 = (bf16[128,1024]{1,0:T(8,128)(2,1)}, bf16[128,1024]{1,0:T(8,128)(2,1)}, u32[]{:S(2)}, u32[]{:S(2)}) collective-permute-start(bf16[128,1024]{1,0:T(8,128)(2,1)} %get-tuple-element.37), channel_id=1, source_target_pairs={{0,252},{1,253},{2,254},{3,255},{4,248},{5,249},{6,250},{7,251},{8... | collective-permute-start | bytes 786440 | tf_op jit(solution)/shard_map/ppermute | solution.py:161
  35.4 23.5 %collective-permute-start.13 = (bf16[128,1024]{1,0:T(8,128)(2,1)}, bf16[128,1024]{1,0:T(8,128)(2,1)}, u32[]{:S(2)}, u32[]{:S(2)}) collective-permute-start(bf16[128,1024]{1,0:T(8,128)(2,1)} %get-tuple-element.38), channel_id=1, source_target_pairs={{0,254},{1,255},{2,248},{3,249},{4,250},{5,251},{6,252},{7,253},{8... | collective-permute-start | bytes 786440 | tf_op jit(solution)/shard_map/ppermute | solution.py:161
  42.2 30.1 %collective-permute-start.4 = (bf16[4,128,512]{2,1,0:T(8,128)(2,1)}, bf16[4,128,512]{2,1,0:T(8,128)(2,1)S(1)}, u32[]{:S(2)}, u32[]{:S(2)}) collective-permute-start(bf16[4,128,512]{2,1,0:T(8,128)(2,1)} %get-tuple-element.51), channel_id=1, source_target_pairs={{0,1},{1,0},{2,3},{3,2},{4,5},{5,4},{6,7},{7,6},{8,9},{9,8},{10,11... | collective-permute-start | bytes 1572872 | tf_op jit(solution)/shard_map/ppermute | solution.py:166
  48.1 22.0 %collective-permute-start = (bf16[128,1024]{1,0:T(8,128)(2,1)}, bf16[128,1024]{1,0:T(8,128)(2,1)}, u32[]{:S(2)}, u32[]{:S(2)}) collective-permute-start(bf16[128,1024]{1,0:T(8,128)(2,1)} %get-tuple-element.27), channel_id=1, source_target_pairs={{0,0},{1,1},{2,2},{3,3},{4,4},{5,5},{6,6},{7,7},{8,8},{9,9},{10,10... | collective-permute-start | bytes 786440 | tf_op jit(solution)/shard_map/ppermute | solution.py:161
  51.3 21.0 %collective-permute-start.1 = (bf16[128,1024]{1,0:T(8,128)(2,1)}, bf16[128,1024]{1,0:T(8,128)(2,1)}, u32[]{:S(2)}, u32[]{:S(2)}) collective-permute-start(bf16[128,1024]{1,0:T(8,128)(2,1)} %get-tuple-element.28), channel_id=1, source_target_pairs={{0,2},{1,3},{2,4},{3,5},{4,6},{5,7},{6,0},{7,1},{8,10},{9,11},{10,... | collective-permute-start | bytes 786440 | tf_op jit(solution)/shard_map/ppermute | solution.py:161
  58.9 13.4 %collective-permute-start.2 = (bf16[128,1024]{1,0:T(8,128)(2,1)}, bf16[128,1024]{1,0:T(8,128)(2,1)}, u32[]{:S(2)}, u32[]{:S(2)}) collective-permute-start(bf16[128,1024]{1,0:T(8,128)(2,1)} %get-tuple-element.29), channel_id=1, source_target_pairs={{0,4},{1,5},{2,6},{3,7},{4,0},{5,1},{6,2},{7,3},{8,12},{9,13},{10,... | collective-permute-start | bytes 786440 | tf_op jit(solution)/shard_map/ppermute | solution.py:161
  60.1 12.2 %collective-permute-start.3 = (bf16[128,1024]{1,0:T(8,128)(2,1)}, bf16[128,1024]{1,0:T(8,128)(2,1)}, u32[]{:S(2)}, u32[]{:S(2)}) collective-permute-start(bf16[128,1024]{1,0:T(8,128)(2,1)} %get-tuple-element.30), channel_id=1, source_target_pairs={{0,6},{1,7},{2,0},{3,1},{4,2},{5,3},{6,4},{7,5},{8,14},{9,15},{10,... | collective-permute-start | bytes 786440 | tf_op jit(solution)/shard_map/ppermute | solution.py:161
  70.2 21.1 %collective-permute-start.19 = (bf16[128,512]{1,0:T(8,128)(2,1)S(1)}, bf16[128,512]{1,0:T(8,128)(2,1)S(1)}, u32[]{:S(2)}, u32[]{:S(2)}) collective-permute-start(bf16[128,512]{1,0:T(8,128)(2,1)S(1)} %get-tuple-element.43), channel_id=1, source_target_pairs={{0,249},{1,248},{2,251},{3,250},{4,253},{5,252},{6,255},{7,254},{8... | collective-permute-start | bytes 393224 | tf_op jit(solution)/shard_map/ppermute | solution.py:161
  78.6 26.7 %collective-permute-start.6 = (bf16[128,1024]{1,0:T(8,128)(2,1)S(1)}, bf16[128,1024]{1,0:T(8,128)(2,1)S(1)}, u32[]{:S(2)}, u32[]{:S(2)}) collective-permute-start(bf16[128,1024]{1,0:T(8,128)(2,1)S(1)} %get-tuple-element.31), channel_id=1, source_target_pairs={{0,8},{1,9},{2,10},{3,11},{4,12},{5,13},{6,14},{7,15},{8,16},{9,17... | collective-permute-start | bytes 786440 | tf_op jit(solution)/shard_map/ppermute | solution.py:161
  81.6 26.7 %collective-permute-start.7 = (bf16[128,1024]{1,0:T(8,128)(2,1)S(1)}, bf16[128,1024]{1,0:T(8,128)(2,1)S(1)}, u32[]{:S(2)}, u32[]{:S(2)}) collective-permute-start(bf16[128,1024]{1,0:T(8,128)(2,1)S(1)} %get-tuple-element.32), channel_id=1, source_target_pairs={{0,10},{1,11},{2,12},{3,13},{4,14},{5,15},{6,8},{7,9},{8,18},{9,19... | collective-permute-start | bytes 786440 | tf_op jit(solution)/shard_map/ppermute | solution.py:161
  83.1 26.5 %collective-permute-start.8 = (bf16[128,1024]{1,0:T(8,128)(2,1)S(1)}, bf16[128,1024]{1,0:T(8,128)(2,1)S(1)}, u32[]{:S(2)}, u32[]{:S(2)}) collective-permute-start(bf16[128,1024]{1,0:T(8,128)(2,1)S(1)} %get-tuple-element.33), channel_id=1, source_target_pairs={{0,12},{1,13},{2,14},{3,15},{4,8},{5,9},{6,10},{7,11},{8,20},{9,21... | collective-permute-start | bytes 786440 | tf_op jit(solution)/shard_map/ppermute | solution.py:161
  86.0 19.2 %collective-permute-start.20 = (bf16[128,512]{1,0:T(8,128)(2,1)S(1)}, bf16[128,512]{1,0:T(8,128)(2,1)S(1)}, u32[]{:S(2)}, u32[]{:S(2)}) collective-permute-start(bf16[128,512]{1,0:T(8,128)(2,1)S(1)} %get-tuple-element.44), channel_id=1, source_target_pairs={{0,251},{1,250},{2,253},{3,252},{4,255},{5,254},{6,249},{7,248},{8... | collective-permute-start | bytes 393224 | tf_op jit(solution)/shard_map/ppermute | solution.py:161
  91.2 14.0 %collective-permute-start.21 = (bf16[128,512]{1,0:T(8,128)(2,1)S(1)}, bf16[128,512]{1,0:T(8,128)(2,1)S(1)}, u32[]{:S(2)}, u32[]{:S(2)}) collective-permute-start(bf16[128,512]{1,0:T(8,128)(2,1)S(1)} %get-tuple-element.45), channel_id=1, source_target_pairs={{0,253},{1,252},{2,255},{3,254},{4,249},{5,248},{6,251},{7,250},{8... | collective-permute-start | bytes 393224 | tf_op jit(solution)/shard_map/ppermute | solution.py:161
  105.3 37.2 %collective-permute-start.15 = (bf16[128,1536]{1,0:T(8,128)(2,1)S(1)}, bf16[128,1536]{1,0:T(8,128)(2,1)S(1)}, u32[]{:S(2)}, u32[]{:S(2)}) collective-permute-start(bf16[128,1536]{1,0:T(8,128)(2,1)S(1)} %get-tuple-element.39), channel_id=1, source_target_pairs={{0,248},{1,249},{2,250},{3,251},{4,252},{5,253},{6,254},{7,255},{8... | collective-permute-start | bytes 1179656 | tf_op jit(solution)/shard_map/ppermute | solution.py:161
  105.3 37.2 %collective-permute-start.16 = (bf16[128,1536]{1,0:T(8,128)(2,1)S(1)}, bf16[128,1536]{1,0:T(8,128)(2,1)S(1)}, u32[]{:S(2)}, u32[]{:S(2)}) collective-permute-start(bf16[128,1536]{1,0:T(8,128)(2,1)S(1)} %get-tuple-element.40), channel_id=1, source_target_pairs={{0,250},{1,251},{2,252},{3,253},{4,254},{5,255},{6,248},{7,249},{8... | collective-permute-start | bytes 1179656 | tf_op jit(solution)/shard_map/ppermute | solution.py:161
  105.3 10.4 %collective-permute-start.9 = (bf16[128,1024]{1,0:T(8,128)(2,1)S(1)}, bf16[128,1024]{1,0:T(8,128)(2,1)S(1)}, u32[]{:S(2)}, u32[]{:S(2)}) collective-permute-start(bf16[128,1024]{1,0:T(8,128)(2,1)S(1)} %get-tuple-element.34), channel_id=1, source_target_pairs={{0,14},{1,15},{2,8},{3,9},{4,10},{5,11},{6,12},{7,13},{8,22},{9,23... | collective-permute-start | bytes 786440 | tf_op jit(solution)/shard_map/ppermute | solution.py:161
  108.2 34.2 %collective-permute-start.17 = (bf16[128,1536]{1,0:T(8,128)(2,1)S(1)}, bf16[128,1536]{1,0:T(8,128)(2,1)S(1)}, u32[]{:S(2)}, u32[]{:S(2)}) collective-permute-start(bf16[128,1536]{1,0:T(8,128)(2,1)S(1)} %get-tuple-element.41), channel_id=1, source_target_pairs={{0,252},{1,253},{2,254},{3,255},{4,248},{5,249},{6,250},{7,251},{8... | collective-permute-start | bytes 1179656 | tf_op jit(solution)/shard_map/ppermute | solution.py:161
  109.6 32.8 %collective-permute-start.18 = (bf16[128,1536]{1,0:T(8,128)(2,1)S(1)}, bf16[128,1536]{1,0:T(8,128)(2,1)S(1)}, u32[]{:S(2)}, u32[]{:S(2)}) collective-permute-start(bf16[128,1536]{1,0:T(8,128)(2,1)S(1)} %get-tuple-element.42), channel_id=1, source_target_pairs={{0,254},{1,255},{2,248},{3,249},{4,250},{5,251},{6,252},{7,253},{8... | collective-permute-start | bytes 1179656 | tf_op jit(solution)/shard_map/ppermute | solution.py:161
  115.7 26.8 %collective-permute-start.22 = (bf16[128,512]{1,0:T(8,128)(2,1)S(1)}, bf16[128,512]{1,0:T(8,128)(2,1)S(1)}, u32[]{:S(2)}, u32[]{:S(2)}) collective-permute-start(bf16[128,512]{1,0:T(8,128)(2,1)S(1)} %get-tuple-element.46), channel_id=1, source_target_pairs={{0,255},{1,254},{2,249},{3,248},{4,251},{5,250},{6,253},{7,252},{8... | collective-permute-start | bytes 393224 | tf_op jit(solution)/shard_map/ppermute | solution.py:161
  (3 other events, 12.3 us)

commit v2 on v1

--- a/solution.py
+++ b/solution.py
@@ -16,6 +16,7 @@
 SLAB_KV = KVH // XS
 QW = SLAB_KV * GROUP * HD
 KW = SLAB_KV * HD
+TOGETHER = 4
 REACH = 4
 MASKED = -1e30
 SCALE = HD**-0.5
@@ -41,12 +42,12 @@
     return rank // 2, rank % 2
 
 
-def vmem_call(body, outs, scratch=()):
+def vmem_call(body, outs, scratch=(), limit=20):
     return pl.pallas_call(
         body,
         out_shape=outs,
         scratch_shapes=scratch,
-        compiler_params=pltpu.CompilerParams(vmem_limit_bytes=20 * 1024 * 1024),
+        compiler_params=pltpu.CompilerParams(vmem_limit_bytes=limit * 1024 * 1024),
     )
 
 
@@ -158,6 +159,9 @@
             for c in range(2 * XS):
                 target = (c // 2 + k) % XS * 2 + (c + flip) % 2
                 pairs.append((p * 2 * XS + c, (p + steps) % count * 2 * XS + target))
+        if all(source == target for source, target in pairs):
+            outs.append(parts[k])
+            continue
         outs.append(lax.ppermute(parts[k], ("pipe", "ctx"), pairs))
     return outs
 
@@ -208,14 +212,14 @@
     bias_ref[:length, :] = jnp.where(seen, F32(0), F32(MASKED))
 
 
-def stacked(ref, i, base):
+def stacked(ref, i, first):
     return jnp.concatenate(
-        [ref[i, :, base + h * HD : base + (h + 1) * HD] for h in range(GROUP)], axis=0
+        [ref[i, :, h * HD : (h + 1) * HD] for h in range(first, first + TOGETHER)], axis=0
     )
 
 
 def probs_of(scores, bias):
-    masked = scores + jnp.concatenate([bias] * GROUP, axis=1)
+    masked = scores + jnp.concatenate([bias] * TOGETHER, axis=1)
     row_max = jnp.max(masked, axis=0, keepdims=True)
     exponent = jnp.exp2((masked - row_max) * F32(EXP2_SCALE))
     return exponent * (1.0 / jnp.sum(exponent, axis=0, keepdims=True))
@@ -232,14 +236,15 @@
         length, start = window_of(i, y)
         first = pl.multiple_of(start * QBLK, QBLK)
         fill_bias(i, y, col_ref, row_ref, bias_ref)
-        for g in range(SLAB_KV):
+        for head in range(0, SLAB_KV * GROUP, TOGETHER):
+            g = head // GROUP
             keys = k_ref[pl.ds(first, length), g * HD : (g + 1) * HD]
             values = v_ref[pl.ds(first, length), g * HD : (g + 1) * HD]
-            queries = stacked(q_ref, i, g * GROUP * HD)
+            queries = stacked(q_ref, i, head)
             weights = probs_of(nt(keys, queries), bias_ref[:length, :]).astype(BF16)
             mixed = tn(values, weights)
-            for h in range(GROUP):
-                col = (g * GROUP + h) * HD
+            for h in range(TOGETHER):
+                col = (head + h) * HD
                 part = mixed[:, h * QBLK : (h + 1) * QBLK].T
                 mixed_ref[i, :, col : col + HD] = part.astype(BF16)
     for k in range(XS):
@@ -259,15 +264,18 @@
             pltpu.VMEM((SEQ // QBLK, 8, QBLK), F32),
             pltpu.VMEM(((REACH + 1) * QBLK, QBLK), F32),
         ),
+        20,
     )(*q, own, other, docs)
 
 
-def backward_body(q_ref, g0, g1, g2, g3, own_ref, other_ref, docs_ref, *refs):
+def backward_body(q0, q1, q2, q3, g0, g1, g2, g3, own_ref, other_ref, docs_ref, *refs):
     mine_refs, theirs_refs = refs[:XS], refs[XS : 2 * XS]
-    g_ref, dq_ref, k_ref, v_ref, col_ref, row_ref, bias_ref, dk_ref, dv_ref = refs[2 * XS :]
+    q_ref, g_ref, dq_ref, k_ref, v_ref = refs[2 * XS : 2 * XS + 5]
+    col_ref, row_ref, bias_ref, dk_ref, dv_ref = refs[2 * XS + 5 :]
     x, y = place()
-    for k, chunk in enumerate((g0, g1, g2, g3)):
-        g_ref[lax.rem(x - k + XS, XS)] = chunk[...]
+    for k, (q_chunk, g_chunk) in enumerate(((q0, g0), (q1, g1), (q2, g2), (q3, g3))):
+        q_ref[lax.rem(x - k + XS, XS)] = q_chunk[...]
+        g_ref[lax.rem(x - k + XS, XS)] = g_chunk[...]
     fill_window(y, 0, own_ref, other_ref, k_ref, v_ref)
     fill_docs(docs_ref, 1, col_ref, row_ref)
     dk_ref[...] = jnp.zeros_like(dk_ref)
@@ -276,11 +284,12 @@
         length, start = window_of(i, y)
         first = pl.multiple_of(start * QBLK, QBLK)
         fill_bias(i, y, col_ref, row_ref, bias_ref)
-        for g in range(SLAB_KV):
+        for head in range(0, SLAB_KV * GROUP, TOGETHER):
+            g = head // GROUP
             span = (pl.ds(first, length), slice(g * HD, (g + 1) * HD))
             keys, values = k_ref[span], v_ref[span]
-            queries = stacked(q_ref, i, g * GROUP * HD)
-            cotan = stacked(g_ref, i, g * GROUP * HD)
+            queries = stacked(q_ref, i, head)
+            cotan = stacked(g_ref, i, head)
             probs = probs_of(nt(keys, queries), bias_ref[:length, :])
             prob_grad = nt(values, cotan)
             delta = jnp.sum(probs * prob_grad, axis=0, keepdims=True)
@@ -288,8 +297,8 @@
             dv_ref[span] += nn(probs.astype(BF16), cotan)
             dk_ref[span] += nn(score_grad, queries)
             dq = tn(keys, score_grad)
-            for h in range(GROUP):
-                col = (g * GROUP + h) * HD
+            for h in range(TOGETHER):
+                col = (head + h) * HD
                 part = dq[:, h * QBLK : (h + 1) * QBLK].T
                 dq_ref[i, :, col : col + HD] = part.astype(BF16)
     for k in range(XS):
@@ -311,6 +320,7 @@
         (
             pltpu.VMEM((XS, QBLK, QW), BF16),
             pltpu.VMEM((XS, QBLK, QW), BF16),
+            pltpu.VMEM((XS, QBLK, QW), BF16),
             pltpu.VMEM((SEQ, KW), BF16),
             pltpu.VMEM((SEQ, KW), BF16),
             pltpu.VMEM((SEQ, QBLK), F32),
@@ -319,7 +329,8 @@
             pltpu.VMEM((SEQ, KW), F32),
             pltpu.VMEM((SEQ, KW), F32),
         ),
-    )(q, *g, own, other, docs)
+        20,
+    )(*q, *g, own, other, docs)
     return outs[:XS], outs[XS:]
 
 
@@ -331,16 +342,16 @@
 def on_device(query_fwd, key_fwd, value_fwd, query_bwd, key_bwd, value_bwd, cotangent, documents):
     own = over_x(cut(key_bwd, value_bwd, key_fwd, value_fwd))
     cotan = sent_turned(turned(cotangent), -1)
-    docs_fwd = shifted(documents, -1)
+    queries_bwd = sent_turned(turned(query_bwd), 0)
     kv_bwd = across(own[:, :, : 2 * KW])
     kv_fwd = across(own[:, :, 2 * KW :])
-    queries_bwd = over_x(cut(query_bwd))
+    docs_fwd = shifted(documents, -1)
     queries_fwd = sent_turned(turned(query_fwd), 0)
     mine, theirs = backward(queries_bwd, cotan, own, kv_bwd, documents)
     mine = sent_turned(mine, -1)
-    theirs = sent_turned(theirs, -1, 1)
     mixed = forward(queries_fwd, own, kv_fwd, docs_fwd)
     mixed = sent_turned(mixed, 1)
+    theirs = sent_turned(theirs, -1, 1)
     return joined(mixed), *joined_grads(mine, theirs)
 
 

time: 144 us -> 131 us (0.910)
  the two profiles are of different devices: /device:TPU:32 before, /device:TPU:64 now
where the time goes in v2:
time: 131 us; the launch traced here: 130 us
  starting transfers between devices  54.4 us (42%)
  waiting for transfers between devices  47.8 us (36%)
  Pallas kernels  26.3 us (20%)
    ppermute x22, starting transfers between devices, sent_turned(): outs.append(lax.ppermute(parts[k], ('pipe', 'ctx'), pairs))  48.2 us
    ppermute x22, waiting for transfers between devices, sent_turned(): outs.append(lax.ppermute(parts[k], ('pipe', 'ctx'), pairs))  43.6 us
    pallas_call x1, Pallas kernels, backward(): vmem_call(backward_body, (jax.ShapeDtypeStruct((QBLK, QW + 2 * KW), BF16)...  10.2 us
    pallas_call x3, Pallas kernels, turned(): pl.pallas_call(turned_body, in_specs=[pl.BlockSpec(memory_space=pl.ANY)],...  6.58 us
    pallas_call x1, Pallas kernels, forward(): vmem_call(forward_body, (jax.ShapeDtypeStruct((QBLK, QW), BF16),) * XS, (...  5.07 us
    all_to_all x1, starting transfers between devices, over_x(): lax.all_to_all(value, 'ctx', split_axis=0, concat_axis=0, axis_index_grou...  4.3 us
    all_to_all x1, waiting for transfers between devices, over_x(): lax.all_to_all(value, 'ctx', split_axis=0, concat_axis=0, axis_index_grou...  4.19 us
  transfers between devices with their start and end apart: 26, of which 8 were waited for; matrix products, arithmetic and copies ran while one was open for 1% of the time, Pallas kernels for 18%

profile of v2, /device:TPU:64, one launch (start us, length us, event | category | flops | bytes accessed | tf_op | source)
XLA Modules:
  0.0 130.4 jit_solution(7854918106098683912)
XLA Ops:
  0.6 2.1 %shard_map.112 = bf16[4,128,1024]{2,1,0:T(8,128)(2,1)} custom-call(bf16[1,128,1024]{2,1,0:T(8,128)(2,1)} %refs_0_.1, bf16[1,128,1024]{2,1,0:T(8,128)(2,1)} %refs_1_.1, bf16[1,128,1024]{2,1,0:T(8,128)(2,1)} %refs_2_.1, bf16[1,128,1024]{2,1,0:T(8,128)(2,1)} %refs_3_.1), custom_call_target="tpu_custom_call" | custom-call | tf_op jit(solution)/shard_map/pallas_call | solution.py:84
  2.8 4.3 %all-to-all-start = ((bf16[4,128,1024]{2,1,0:T(8,128)(2,1)}), bf16[4,128,1024]{2,1,0:T(8,128)(2,1)S(1)}, u32[]{:S(2)}, u32[]{:S(2)}) async-start(bf16[4,128,1024]{2,1,0:T(8,128)(2,1)} %shard_map.112), calls=%async_computation | async-start | bytes 2097152 | tf_op jit(solution)/shard_map/all_to_all | solution.py:176
  7.1 2.2 %shard_map.115 = (bf16[128,1024]{1,0:T(8,128)(2,1)}, bf16[128,1024]{1,0:T(8,128)(2,1)}, bf16[128,1024]{1,0:T(8,128)(2,1)}, bf16[128,1024]{1,0:T(8,128)(2,1)}) custom-call(bf16[1,128,4096]{2,1,0:T(8,128)(2,1)} %in_ref.4), custom_call_target="tpu_custom_call" | custom-call | tf_op jit(solution)/shard_map/pallas_call | solution.py:113
  9.3 3.6 %collective-permute-start.10 = (bf16[128,1024]{1,0:T(8,128)(2,1)}, bf16[128,1024]{1,0:T(8,128)(2,1)S(1)}, u32[]{:S(2)}, u32[]{:S(2)}) collective-permute-start(bf16[128,1024]{1,0:T(8,128)(2,1)} %get-tuple-element.41), channel_id=1, source_target_pairs={{0,4},{1,5},{2,6},{3,7},{4,0},{5,1},{6,2},{7,3},{8,12},{9,13},{10,... | collective-permute-start | bytes 786440 | tf_op jit(solution)/shard_map/ppermute | solution.py:165
  14.0 2.2 %shard_map.116 = (bf16[128,1024]{1,0:T(8,128)(2,1)}, bf16[128,1024]{1,0:T(8,128)(2,1)}, bf16[128,1024]{1,0:T(8,128)(2,1)}, bf16[128,1024]{1,0:T(8,128)(2,1)}) custom-call(bf16[1,128,4096]{2,1,0:T(8,128)(2,1)} %in_ref.5), custom_call_target="tpu_custom_call" | custom-call | tf_op jit(solution)/shard_map/pallas_call | solution.py:113
  17.4 2.1 %collective-permute-start.13 = (bf16[128,1024]{1,0:T(8,128)(2,1)}, bf16[128,1024]{1,0:T(8,128)(2,1)S(1)}, u32[]{:S(2)}, u32[]{:S(2)}) collective-permute-start(bf16[128,1024]{1,0:T(8,128)(2,1)} %get-tuple-element.44), channel_id=1, source_target_pairs={{0,250},{1,251},{2,252},{3,253},{4,254},{5,255},{6,248},{7,249},{8... | collective-permute-start | bytes 786440 | tf_op jit(solution)/shard_map/ppermute | solution.py:165
  19.5 4.2 %all-to-all-done.own_ref = bf16[4,128,1024]{2,1,0:T(8,128)(2,1)S(1)} async-done(((bf16[4,128,1024]{2,1,0:T(8,128)(2,1)}), bf16[4,128,1024]{2,1,0:T(8,128)(2,1)S(1)}, u32[]{:S(2)}, u32[]{:S(2)}) %all-to-all-start) | async-done | bytes 1048608 | tf_op jit(solution)/shard_map/all_to_all | solution.py:176
  24.7 1.6 %collective-permute-start.16 = (bf16[4,128,512]{2,1,0:T(8,128)(2,1)}, bf16[4,128,512]{2,1,0:T(8,128)(2,1)S(1)}, u32[]{:S(2)}, u32[]{:S(2)}) collective-permute-start(bf16[4,128,512]{2,1,0:T(8,128)(2,1)} %get-tuple-element.58), channel_id=1, source_target_pairs={{0,1},{1,0},{2,3},{3,2},{4,5},{5,4},{6,7},{7,6},{8,9},{9,8},{10,11... | collective-permute-start | bytes 1572872 | tf_op jit(solution)/shard_map/ppermute | solution.py:170
  26.3 5.8 %collective-permute-done.10.q2 = bf16[128,1024]{1,0:T(8,128)(2,1)S(1)} collective-permute-done((bf16[128,1024]{1,0:T(8,128)(2,1)}, bf16[128,1024]{1,0:T(8,128)(2,1)S(1)}, u32[]{:S(2)}, u32[]{:S(2)}) %collective-permute-start.10) | collective-permute-done | bytes 262176 | tf_op jit(solution)/shard_map/ppermute | solution.py:165
  32.1 3.0 %collective-permute-start.15 = (bf16[128,1024]{1,0:T(8,128)(2,1)}, bf16[128,1024]{1,0:T(8,128)(2,1)}, u32[]{:S(2)}, u32[]{:S(2)}) collective-permute-start(bf16[128,1024]{1,0:T(8,128)(2,1)} %get-tuple-element.46), channel_id=1, source_target_pairs={{0,254},{1,255},{2,248},{3,249},{4,250},{5,251},{6,252},{7,253},{8... | collective-permute-start | bytes 786440 | tf_op jit(solution)/shard_map/ppermute | solution.py:165
  35.4 2.2 %shard_map.111 = (bf16[128,1024]{1,0:T(8,128)(2,1)}, bf16[128,1024]{1,0:T(8,128)(2,1)}, bf16[128,1024]{1,0:T(8,128)(2,1)}, bf16[128,1024]{1,0:T(8,128)(2,1)}) custom-call(bf16[1,128,4096]{2,1,0:T(8,128)(2,1)} %in_ref.3), custom_call_target="tpu_custom_call" | custom-call | tf_op jit(solution)/shard_map/pallas_call | solution.py:113
  37.6 7.2 %collective-permute-done.14.g2 = bf16[128,1024]{1,0:T(8,128)(2,1)} collective-permute-done((bf16[128,1024]{1,0:T(8,128)(2,1)}, bf16[128,1024]{1,0:T(8,128)(2,1)}, u32[]{:S(2)}, u32[]{:S(2)}) %collective-permute-start.14) | collective-permute-done | bytes 262176 | tf_op jit(solution)/shard_map/ppermute | solution.py:165
  44.8 2.7 %collective-permute-start.1 = (bf16[128,1024]{1,0:T(8,128)(2,1)}, bf16[128,1024]{1,0:T(8,128)(2,1)S(1)}, u32[]{:S(2)}, u32[]{:S(2)}) collective-permute-start(bf16[128,1024]{1,0:T(8,128)(2,1)} %get-tuple-element.33), channel_id=1, source_target_pairs={{0,4},{1,5},{2,6},{3,7},{4,0},{5,1},{6,2},{7,3},{8,12},{9,13},{10,... | collective-permute-start | bytes 786440 | tf_op jit(solution)/shard_map/ppermute | solution.py:165
  49.6 10.2 %shard_map.117 = (bf16[128,1536]{1,0:T(8,128)(2,1)S(1)}, bf16[128,1536]{1,0:T(8,128)(2,1)S(1)}, bf16[128,1536]{1,0:T(8,128)(2,1)S(1)}, bf16[128,1536]{1,0:T(8,12...) custom-call(bf16[128,1024]{1,0:T(8,128)(2,1)S(1)} %copy-done, ...), custom_call_target="tpu_custom_call" | custom-call | tf_op jit(solution)/shard_map/pallas_call | solution.py:316
  61.7 5.1 %shard_map.113 = (bf16[128,1024]{1,0:T(8,128)(2,1)S(1)}, bf16[128,1024]{1,0:T(8,128)(2,1)S(1)}, bf16[128,1024]{1,0:T(8,128)(2,1)S(1)}, bf16[128,1024]{1,0:T(8,128)(2,1)S(1)}) custom-call(bf16[128,1024]{1,0:T(8,128)(2,1)S(1)} %copy-done.1, bf16[128,1024]{1,0:T(8,128)(2,1)S(1)} %collective-permute-done.q1, bf16[128,1024]{1,0:T(8,128)(2,1)S(1)} %collective-permute-done.1.q2, ...), custom_call_target="tpu_custom_call" | custom-call | tf_op jit(solution)/shard_map/pallas_call | solution.py:255
  68.3 3.1 %collective-permute-start.7 = (bf16[128,1024]{1,0:T(8,128)(2,1)S(1)}, bf16[128,1024]{1,0:T(8,128)(2,1)S(1)}, u32[]{:S(2)}, u32[]{:S(2)}) collective-permute-start(bf16[128,1024]{1,0:T(8,128)(2,1)S(1)} %get-tuple-element.37), channel_id=1, source_target_pairs={{0,12},{1,13},{2,14},{3,15},{4,8},{5,9},{6,10},{7,11},{8,20},{9,21... | collective-permute-start | bytes 786440 | tf_op jit(solution)/shard_map/ppermute | solution.py:165
  71.3 4.1 %collective-permute-start.22 = (bf16[128,512]{1,0:T(8,128)(2,1)S(1)}, bf16[128,512]{1,0:T(8,128)(2,1)S(1)}, u32[]{:S(2)}, u32[]{:S(2)}) collective-permute-start(bf16[128,512]{1,0:T(8,128)(2,1)S(1)} %get-tuple-element.52), channel_id=1, source_target_pairs={{0,251},{1,250},{2,253},{3,252},{4,255},{5,254},{6,249},{7,248},{8... | collective-permute-start | bytes 393224 | tf_op jit(solution)/shard_map/ppermute | solution.py:165
  76.1 14.1 %collective-permute-done.22.refs_5_ = bf16[128,512]{1,0:T(8,128)(2,1)S(1)} collective-permute-done((bf16[128,512]{1,0:T(8,128)(2,1)S(1)}, bf16[128,512]{1,0:T(8,128)(2,1)S(1)}, u32[]{:S(2)}, u32[]{:S(2)}) %collective-permute-start.22) | collective-permute-done | bytes 131104 | tf_op jit(solution)/shard_map/ppermute | solution.py:165
  90.3 2.9 %collective-permute-start.8 = (bf16[128,1024]{1,0:T(8,128)(2,1)S(1)}, bf16[128,1024]{1,0:T(8,128)(2,1)S(1)}, u32[]{:S(2)}, u32[]{:S(2)}) collective-permute-start(bf16[128,1024]{1,0:T(8,128)(2,1)S(1)} %get-tuple-element.38), channel_id=1, source_target_pairs={{0,14},{1,15},{2,8},{3,9},{4,10},{5,11},{6,12},{7,13},{8,22},{9,23... | collective-permute-start | bytes 786440 | tf_op jit(solution)/shard_map/ppermute | solution.py:165
  93.2 3.1 %collective-permute-start.19 = (bf16[128,1536]{1,0:T(8,128)(2,1)S(1)}, bf16[128,1536]{1,0:T(8,128)(2,1)S(1)}, u32[]{:S(2)}, u32[]{:S(2)}) collective-permute-start(bf16[128,1536]{1,0:T(8,128)(2,1)S(1)} %get-tuple-element.49), channel_id=1, source_target_pairs={{0,252},{1,253},{2,254},{3,255},{4,248},{5,249},{6,250},{7,251},{8... | collective-permute-start | bytes 1179656 | tf_op jit(solution)/shard_map/ppermute | solution.py:165
  96.3 1.5 %collective-permute-start.20 = (bf16[128,1536]{1,0:T(8,128)(2,1)S(1)}, bf16[128,1536]{1,0:T(8,128)(2,1)S(1)}, u32[]{:S(2)}, u32[]{:S(2)}) collective-permute-start(bf16[128,1536]{1,0:T(8,128)(2,1)S(1)} %get-tuple-element.50), channel_id=1, source_target_pairs={{0,254},{1,255},{2,248},{3,249},{4,250},{5,251},{6,252},{7,253},{8... | collective-permute-start | bytes 1179656 | tf_op jit(solution)/shard_map/ppermute | solution.py:165
  97.8 1.8 %collective-permute-done.8.refs_3_ = bf16[128,1024]{1,0:T(8,128)(2,1)S(1)} collective-permute-done((bf16[128,1024]{1,0:T(8,128)(2,1)S(1)}, bf16[128,1024]{1,0:T(8,128)(2,1)S(1)}, u32[]{:S(2)}, u32[]{:S(2)}) %collective-permute-start.8) | collective-permute-done | bytes 262176 | tf_op jit(solution)/shard_map/ppermute | solution.py:165
  99.6 14.8 %collective-permute-start.24 = (bf16[128,512]{1,0:T(8,128)(2,1)S(1)}, bf16[128,512]{1,0:T(8,128)(2,1)S(1)}, u32[]{:S(2)}, u32[]{:S(2)}) collective-permute-start(bf16[128,512]{1,0:T(8,128)(2,1)S(1)} %get-tuple-element.54), channel_id=1, source_target_pairs={{0,255},{1,254},{2,249},{3,248},{4,251},{5,250},{6,253},{7,252},{8... | collective-permute-start | bytes 393224 | tf_op jit(solution)/shard_map/ppermute | solution.py:165
  115.5 13.6 %collective-permute-done.24.refs_7_ = bf16[128,512]{1,0:T(8,128)(2,1)S(1)} collective-permute-done((bf16[128,512]{1,0:T(8,128)(2,1)S(1)}, bf16[128,512]{1,0:T(8,128)(2,1)S(1)}, u32[]{:S(2)}, u32[]{:S(2)}) %collective-permute-start.24) | collective-permute-done | bytes 131104 | tf_op jit(solution)/shard_map/ppermute | solution.py:165
  (43 shorter events, 12.1 us)
Async XLA Ops:
  2.8 20.9 %all-to-all-start = ((bf16[4,128,1024]{2,1,0:T(8,128)(2,1)}), bf16[4,128,1024]{2,1,0:T(8,128)(2,1)S(1)}, u32[]{:S(2)}, u32[]{:S(2)}) async-start(bf16[4,128,1024]{2,1,0:T(8,128)(2,1)} %shard_map.112), calls=%async_computation | async-start | bytes 2097152 | tf_op jit(solution)/shard_map/all_to_all | solution.py:176
  9.3 22.8 %collective-permute-start.10 = (bf16[128,1024]{1,0:T(8,128)(2,1)}, bf16[128,1024]{1,0:T(8,128)(2,1)S(1)}, u32[]{:S(2)}, u32[]{:S(2)}) collective-permute-start(bf16[128,1024]{1,0:T(8,128)(2,1)} %get-tuple-element.41), channel_id=1, source_target_pairs={{0,4},{1,5},{2,6},{3,7},{4,0},{5,1},{6,2},{7,3},{8,12},{9,13},{10,... | collective-permute-start | bytes 786440 | tf_op jit(solution)/shard_map/ppermute | solution.py:165
  12.9 19.2 %collective-permute-start.11 = (bf16[128,1024]{1,0:T(8,128)(2,1)}, bf16[128,1024]{1,0:T(8,128)(2,1)S(1)}, u32[]{:S(2)}, u32[]{:S(2)}) collective-permute-start(bf16[128,1024]{1,0:T(8,128)(2,1)} %get-tuple-element.42), channel_id=1, source_target_pairs={{0,6},{1,7},{2,0},{3,1},{4,2},{5,3},{6,4},{7,5},{8,14},{9,15},{10,... | collective-permute-start | bytes 786440 | tf_op jit(solution)/shard_map/ppermute | solution.py:165
  16.3 18.9 %collective-permute-start.12 = (bf16[128,1024]{1,0:T(8,128)(2,1)}, bf16[128,1024]{1,0:T(8,128)(2,1)S(1)}, u32[]{:S(2)}, u32[]{:S(2)}) collective-permute-start(bf16[128,1024]{1,0:T(8,128)(2,1)} %get-tuple-element.43), channel_id=1, source_target_pairs={{0,248},{1,249},{2,250},{3,251},{4,252},{5,253},{6,254},{7,255},{8... | collective-permute-start | bytes 786440 | tf_op jit(solution)/shard_map/ppermute | solution.py:165
  17.4 17.7 %collective-permute-start.13 = (bf16[128,1024]{1,0:T(8,128)(2,1)}, bf16[128,1024]{1,0:T(8,128)(2,1)S(1)}, u32[]{:S(2)}, u32[]{:S(2)}) collective-permute-start(bf16[128,1024]{1,0:T(8,128)(2,1)} %get-tuple-element.44), channel_id=1, source_target_pairs={{0,250},{1,251},{2,252},{3,253},{4,254},{5,255},{6,248},{7,249},{8... | collective-permute-start | bytes 786440 | tf_op jit(solution)/shard_map/ppermute | solution.py:165
  24.7 24.8 %collective-permute-start.16 = (bf16[4,128,512]{2,1,0:T(8,128)(2,1)}, bf16[4,128,512]{2,1,0:T(8,128)(2,1)S(1)}, u32[]{:S(2)}, u32[]{:S(2)}) collective-permute-start(bf16[4,128,512]{2,1,0:T(8,128)(2,1)} %get-tuple-element.58), channel_id=1, source_target_pairs={{0,1},{1,0},{2,3},{3,2},{4,5},{5,4},{6,7},{7,6},{8,9},{9,8},{10,11... | collective-permute-start | bytes 1572872 | tf_op jit(solution)/shard_map/ppermute | solution.py:170
  32.1 12.7 %collective-permute-start.14 = (bf16[128,1024]{1,0:T(8,128)(2,1)}, bf16[128,1024]{1,0:T(8,128)(2,1)}, u32[]{:S(2)}, u32[]{:S(2)}) collective-permute-start(bf16[128,1024]{1,0:T(8,128)(2,1)} %get-tuple-element.45), channel_id=1, source_target_pairs={{0,252},{1,253},{2,254},{3,255},{4,248},{5,249},{6,250},{7,251},{8... | collective-permute-start | bytes 786440 | tf_op jit(solution)/shard_map/ppermute | solution.py:165
  32.1 12.7 %collective-permute-start.15 = (bf16[128,1024]{1,0:T(8,128)(2,1)}, bf16[128,1024]{1,0:T(8,128)(2,1)}, u32[]{:S(2)}, u32[]{:S(2)}) collective-permute-start(bf16[128,1024]{1,0:T(8,128)(2,1)} %get-tuple-element.46), channel_id=1, source_target_pairs={{0,254},{1,255},{2,248},{3,249},{4,250},{5,251},{6,252},{7,253},{8... | collective-permute-start | bytes 786440 | tf_op jit(solution)/shard_map/ppermute | solution.py:165
  35.1 13.0 %collective-permute-start.9 = (bf16[128,1024]{1,0:T(8,128)(2,1)}, bf16[128,1024]{1,0:T(8,128)(2,1)}, u32[]{:S(2)}, u32[]{:S(2)}) collective-permute-start(bf16[128,1024]{1,0:T(8,128)(2,1)} %get-tuple-element.40), channel_id=1, source_target_pairs={{0,2},{1,3},{2,4},{3,5},{4,6},{5,7},{6,0},{7,1},{8,10},{9,11},{10,... | collective-permute-start | bytes 786440 | tf_op jit(solution)/shard_map/ppermute | solution.py:165
  35.2 26.5 %collective-permute-start.3 = (bf16[4,128,512]{2,1,0:T(8,128)(2,1)}, bf16[4,128,512]{2,1,0:T(8,128)(2,1)S(1)}, u32[]{:S(2)}, u32[]{:S(2)}) collective-permute-start(bf16[4,128,512]{2,1,0:T(8,128)(2,1)} %get-tuple-element.59), channel_id=1, source_target_pairs={{0,1},{1,0},{2,3},{3,2},{4,5},{5,4},{6,7},{7,6},{8,9},{9,8},{10,11... | collective-permute-start | bytes 1572872 | tf_op jit(solution)/shard_map/ppermute | solution.py:170
  44.8 16.4 %collective-permute-start = (bf16[128,1024]{1,0:T(8,128)(2,1)}, bf16[128,1024]{1,0:T(8,128)(2,1)S(1)}, u32[]{:S(2)}, u32[]{:S(2)}) collective-permute-start(bf16[128,1024]{1,0:T(8,128)(2,1)} %get-tuple-element.32), channel_id=1, source_target_pairs={{0,2},{1,3},{2,4},{3,5},{4,6},{5,7},{6,0},{7,1},{8,10},{9,11},{10,... | collective-permute-start | bytes 786440 | tf_op jit(solution)/shard_map/ppermute | solution.py:165
  44.8 16.4 %collective-permute-start.1 = (bf16[128,1024]{1,0:T(8,128)(2,1)}, bf16[128,1024]{1,0:T(8,128)(2,1)S(1)}, u32[]{:S(2)}, u32[]{:S(2)}) collective-permute-start(bf16[128,1024]{1,0:T(8,128)(2,1)} %get-tuple-element.33), channel_id=1, source_target_pairs={{0,4},{1,5},{2,6},{3,7},{4,0},{5,1},{6,2},{7,3},{8,12},{9,13},{10,... | collective-permute-start | bytes 786440 | tf_op jit(solution)/shard_map/ppermute | solution.py:165
  48.1 13.5 %collective-permute-start.2 = (bf16[128,1024]{1,0:T(8,128)(2,1)}, bf16[128,1024]{1,0:T(8,128)(2,1)S(1)}, u32[]{:S(2)}, u32[]{:S(2)}) collective-permute-start(bf16[128,1024]{1,0:T(8,128)(2,1)} %get-tuple-element.34), channel_id=1, source_target_pairs={{0,6},{1,7},{2,0},{3,1},{4,2},{5,3},{6,4},{7,5},{8,14},{9,15},{10,... | collective-permute-start | bytes 786440 | tf_op jit(solution)/shard_map/ppermute | solution.py:165
  59.8 15.6 %collective-permute-start.21 = (bf16[128,512]{1,0:T(8,128)(2,1)S(1)}, bf16[128,512]{1,0:T(8,128)(2,1)S(1)}, u32[]{:S(2)}, u32[]{:S(2)}) collective-permute-start(bf16[128,512]{1,0:T(8,128)(2,1)S(1)} %get-tuple-element.51), channel_id=1, source_target_pairs={{0,249},{1,248},{2,251},{3,250},{4,253},{5,252},{6,255},{7,254},{8... | collective-permute-start | bytes 393224 | tf_op jit(solution)/shard_map/ppermute | solution.py:165
  66.8 23.5 %collective-permute-start.5 = (bf16[128,1024]{1,0:T(8,128)(2,1)S(1)}, bf16[128,1024]{1,0:T(8,128)(2,1)S(1)}, u32[]{:S(2)}, u32[]{:S(2)}) collective-permute-start(bf16[128,1024]{1,0:T(8,128)(2,1)S(1)} %get-tuple-element.35), channel_id=1, source_target_pairs={{0,8},{1,9},{2,10},{3,11},{4,12},{5,13},{6,14},{7,15},{8,16},{9,17... | collective-permute-start | bytes 786440 | tf_op jit(solution)/shard_map/ppermute | solution.py:165
  66.9 26.4 %collective-permute-start.6 = (bf16[128,1024]{1,0:T(8,128)(2,1)S(1)}, bf16[128,1024]{1,0:T(8,128)(2,1)S(1)}, u32[]{:S(2)}, u32[]{:S(2)}) collective-permute-start(bf16[128,1024]{1,0:T(8,128)(2,1)S(1)} %get-tuple-element.36), channel_id=1, source_target_pairs={{0,10},{1,11},{2,12},{3,13},{4,14},{5,15},{6,8},{7,9},{8,18},{9,19... | collective-permute-start | bytes 786440 | tf_op jit(solution)/shard_map/ppermute | solution.py:165
  68.3 28.0 %collective-permute-start.7 = (bf16[128,1024]{1,0:T(8,128)(2,1)S(1)}, bf16[128,1024]{1,0:T(8,128)(2,1)S(1)}, u32[]{:S(2)}, u32[]{:S(2)}) collective-permute-start(bf16[128,1024]{1,0:T(8,128)(2,1)S(1)} %get-tuple-element.37), channel_id=1, source_target_pairs={{0,12},{1,13},{2,14},{3,15},{4,8},{5,9},{6,10},{7,11},{8,20},{9,21... | collective-permute-start | bytes 786440 | tf_op jit(solution)/shard_map/ppermute | solution.py:165
  71.3 18.9 %collective-permute-start.22 = (bf16[128,512]{1,0:T(8,128)(2,1)S(1)}, bf16[128,512]{1,0:T(8,128)(2,1)S(1)}, u32[]{:S(2)}, u32[]{:S(2)}) collective-permute-start(bf16[128,512]{1,0:T(8,128)(2,1)S(1)} %get-tuple-element.52), channel_id=1, source_target_pairs={{0,251},{1,250},{2,253},{3,252},{4,255},{5,254},{6,249},{7,248},{8... | collective-permute-start | bytes 393224 | tf_op jit(solution)/shard_map/ppermute | solution.py:165
  75.4 14.8 %collective-permute-start.23 = (bf16[128,512]{1,0:T(8,128)(2,1)S(1)}, bf16[128,512]{1,0:T(8,128)(2,1)S(1)}, u32[]{:S(2)}, u32[]{:S(2)}) collective-permute-start(bf16[128,512]{1,0:T(8,128)(2,1)S(1)} %get-tuple-element.53), channel_id=1, source_target_pairs={{0,253},{1,252},{2,255},{3,254},{4,249},{5,248},{6,251},{7,250},{8... | collective-permute-start | bytes 393224 | tf_op jit(solution)/shard_map/ppermute | solution.py:165
  90.2 38.9 %collective-permute-start.17 = (bf16[128,1536]{1,0:T(8,128)(2,1)S(1)}, bf16[128,1536]{1,0:T(8,128)(2,1)S(1)}, u32[]{:S(2)}, u32[]{:S(2)}) collective-permute-start(bf16[128,1536]{1,0:T(8,128)(2,1)S(1)} %get-tuple-element.47), channel_id=1, source_target_pairs={{0,248},{1,249},{2,250},{3,251},{4,252},{5,253},{6,254},{7,255},{8... | collective-permute-start | bytes 1179656 | tf_op jit(solution)/shard_map/ppermute | solution.py:165
  90.2 38.8 %collective-permute-start.18 = (bf16[128,1536]{1,0:T(8,128)(2,1)S(1)}, bf16[128,1536]{1,0:T(8,128)(2,1)S(1)}, u32[]{:S(2)}, u32[]{:S(2)}) collective-permute-start(bf16[128,1536]{1,0:T(8,128)(2,1)S(1)} %get-tuple-element.48), channel_id=1, source_target_pairs={{0,250},{1,251},{2,252},{3,253},{4,254},{5,255},{6,248},{7,249},{8... | collective-permute-start | bytes 1179656 | tf_op jit(solution)/shard_map/ppermute | solution.py:165
  93.2 35.9 %collective-permute-start.19 = (bf16[128,1536]{1,0:T(8,128)(2,1)S(1)}, bf16[128,1536]{1,0:T(8,128)(2,1)S(1)}, u32[]{:S(2)}, u32[]{:S(2)}) collective-permute-start(bf16[128,1536]{1,0:T(8,128)(2,1)S(1)} %get-tuple-element.49), channel_id=1, source_target_pairs={{0,252},{1,253},{2,254},{3,255},{4,248},{5,249},{6,250},{7,251},{8... | collective-permute-start | bytes 1179656 | tf_op jit(solution)/shard_map/ppermute | solution.py:165
  96.3 32.8 %collective-permute-start.20 = (bf16[128,1536]{1,0:T(8,128)(2,1)S(1)}, bf16[128,1536]{1,0:T(8,128)(2,1)S(1)}, u32[]{:S(2)}, u32[]{:S(2)}) collective-permute-start(bf16[128,1536]{1,0:T(8,128)(2,1)S(1)} %get-tuple-element.50), channel_id=1, source_target_pairs={{0,254},{1,255},{2,248},{3,249},{4,250},{5,251},{6,252},{7,253},{8... | collective-permute-start | bytes 1179656 | tf_op jit(solution)/shard_map/ppermute | solution.py:165
  99.6 29.5 %collective-permute-start.24 = (bf16[128,512]{1,0:T(8,128)(2,1)S(1)}, bf16[128,512]{1,0:T(8,128)(2,1)S(1)}, u32[]{:S(2)}, u32[]{:S(2)}) collective-permute-start(bf16[128,512]{1,0:T(8,128)(2,1)S(1)} %get-tuple-element.54), channel_id=1, source_target_pairs={{0,255},{1,254},{2,249},{3,248},{4,251},{5,250},{6,253},{7,252},{8... | collective-permute-start | bytes 393224 | tf_op jit(solution)/shard_map/ppermute | solution.py:165
  (5 other events, 60.5 us)
